TPU v7x, 128 devices: a whole 4x4x4 slice. The times are simulated.
128 devices in a mesh: shard: 32 (over z, y, x_lo), model: 4 (over x_hi, core).
Axes of the slice: x: 4 (x_hi: 2, x_lo: 2; x = x_hi * 2 + x_lo), y: 4, z: 4, core: 2. Of those that a mesh axis runs over, the one named last changes fastest.
Arguments:
- w_query: bfloat16 [12288, 12288], P('shard', 'model'), may hold values from -0.109375 to 0.109375
- low_query: bfloat16 [12288, 16], P('shard'), may hold values from -0.0546875 to 0.0546875
- high_query: bfloat16 [16, 12288], P(None, 'model'), may hold values from -1.5 to 1.5
- w_key: bfloat16 [12288, 12288], P('shard', 'model'), may hold values from -0.109375 to 0.109375
- low_key: bfloat16 [12288, 16], P('shard'), may hold values from -0.0546875 to 0.0546875
- high_key: bfloat16 [16, 12288], P(None, 'model'), may hold values from -1.5 to 1.5
- w_value: bfloat16 [12288, 12288], P('shard', 'model'), may hold values from -0.109375 to 0.109375
- low_value: bfloat16 [12288, 16], P('shard'), may hold values from -0.0546875 to 0.0546875
- high_value: bfloat16 [16, 12288], P(None, 'model'), may hold values from -1.5 to 1.5
- norm_gain: float32 [12288], P('shard'), may hold values from 0.25 to 1.75
Outputs:
- final_query: bfloat16 [12288, 12288], P(None, ('model', 'shard'))
- final_key: bfloat16 [12288, 12288], P(None, ('model', 'shard'))
- final_value: bfloat16 [12288, 12288], P(None, ('model', 'shard'))
- scale_query: float32 [12288], P(('model', 'shard'))
- scale_key: float32 [12288], P(('model', 'shard'))
- scale_value: float32 [12288], P(('model', 'shard'))
All inputs are finite; a program needn't handle non-finite values. Where the computation divides by a largest or mean magnitude, that divisor is 1e-20 or more.
Results may differ from a plain program's by a relative error of at most 0.001.
Values may be sent and summed in bfloat16 or wider, within the bound.
No kernel may reach another device: no remote copies, remote signals or barrier semaphores. Data moves between devices by JAX's collectives and lax.ppermute only.
A program may use at most 128 MiB of HBM per device.

v0:
```python
import jax
import jax.numpy as jnp
from jax import lax
from jax.sharding import PartitionSpec as P

mix_rate = 1.0


def sent_to_all(value, axis):
    copies = jnp.broadcast_to(value, (lax.axis_size(axis), *value.shape))
    return lax.all_to_all(copies, axis, split_axis=0, concat_axis=0, tiled=True)


def over_copies(value, axis):
    everything = sent_to_all(value, axis)
    return jnp.max(everything, axis=0)


def together(arrays, axis):
    line, at, done = (jnp.concatenate([a.reshape(-1) for a in arrays]), 0, [])
    so_far = over_copies(line, axis)
    for a in arrays:
        done.append(so_far[at : at + a.size].reshape(a.shape))
        at += a.size
    return tuple(done)


def on_device(
    w_query,
    low_query,
    high_query,
    w_key,
    low_key,
    high_key,
    w_value,
    low_value,
    high_value,
    norm_gain,
):
    result_query = w_query.astype(jnp.float32) + mix_rate * jnp.dot(
        low_query, high_query, preferred_element_type=jnp.float32
    )
    result_key = w_key.astype(jnp.float32) + mix_rate * jnp.dot(
        low_key, high_key, preferred_element_type=jnp.float32
    )
    result_value = w_value.astype(jnp.float32) + mix_rate * jnp.dot(
        low_value, high_value, preferred_element_type=jnp.float32
    )
    result_gained_query = result_query * norm_gain[:, None]
    result_gained_key = result_key * norm_gain[:, None]
    result_gained_value = result_value * norm_gain[:, None]
    scale_query, scale_key, scale_value = together(
        (
            jnp.max(jnp.abs(result_gained_query), axis=0),
            jnp.max(jnp.abs(result_gained_key), axis=0),
            jnp.max(jnp.abs(result_gained_value), axis=0),
        ),
        "shard",
    )
    narrow_query, narrow_key, narrow_value = (
        (result_gained_query / scale_query).astype(jnp.bfloat16),
        (result_gained_key / scale_key).astype(jnp.bfloat16),
        (result_gained_value / scale_value).astype(jnp.bfloat16),
    )
    final_query, final_key, final_value = (
        lax.all_to_all(narrow_query, "shard", split_axis=1, concat_axis=0, tiled=True),
        lax.all_to_all(narrow_key, "shard", split_axis=1, concat_axis=0, tiled=True),
        lax.all_to_all(narrow_value, "shard", split_axis=1, concat_axis=0, tiled=True),
    )
    place = lax.axis_index("shard")
    scale_query = lax.dynamic_slice_in_dim(
        scale_query, place * final_query.shape[1], final_query.shape[1]
    )
    scale_key = lax.dynamic_slice_in_dim(scale_key, place * final_key.shape[1], final_key.shape[1])
    scale_value = lax.dynamic_slice_in_dim(
        scale_value, place * final_value.shape[1], final_value.shape[1]
    )
    return (final_query, final_key, final_value, scale_query, scale_key, scale_value)


def solution(mesh):
    return jax.shard_map(
        on_device,
        mesh=mesh,
        in_specs=(
            P("shard", "model"),
            P("shard", None),
            P(None, "model"),
            P("shard", "model"),
            P("shard", None),
            P(None, "model"),
            P("shard", "model"),
            P("shard", None),
            P(None, "model"),
            P("shard"),
        ),
        out_specs=(
            P(None, ("model", "shard")),
            P(None, ("model", "shard")),
            P(None, ("model", "shard")),
            P(("model", "shard")),
            P(("model", "shard")),
            P(("model", "shard")),
        ),
        check_vma=False,
    )
```

profile of v0, /device:TPU:0, one launch (start us, length us, event | category | flops | bytes accessed | tf_op | source)
XLA Modules:
  0.0 155.9 jit_solution(16265798905348577380)
XLA Ops:
  0.6 0.0 copy-start
  0.6 0.0 copy-start.5
  0.7 0.0 copy-start.6
  0.7 0.8 copy-done
  1.5 4.6 %abs_reduce_fusion.2 = (f32[3072]{0:T(1024)S(1)}, f32[384,3072]{1,0:T(8,128)}) fusion(f32[384]{0:T(512)} %param.19, bf16[384,16]{0,1:T(8,128)(2,1)} %param.11, bf16[16,3072]{1,0:T(8,128)(2,1)S(1)} %copy-done, bf16[384,3072]{1,0:T(8,128)(2,1)} %param.10), kind=kOutput, calls=%fused_computation.7 | convolution fusion | flops 43643904 | bytes 7202304 | tf_op jit(solution)/shard_map/dot_general | solution.py:40
  6.2 0.0 copy-done.1
  6.2 0.0 copy-start.2
  6.2 0.0 copy-start.4
  6.2 0.0 copy-start.7
  6.2 3.0 %abs_reduce_fusion = (f32[3072]{0:T(1024)S(1)}, f32[384,3072]{1,0:T(8,128)}) fusion(f32[384]{0:T(512)S(1)} %copy-done.5, bf16[384,16]{0,1:T(8,128)(2,1)S(1)} %copy-done.6, bf16[16,3072]{1,0:T(8,128)(2,1)S(1)} %copy-done.3, bf16[384,3072]{1,0:T(8,128)(2,1)S(1)} %copy-done.1), kind=kOutput, calls=%fused_computation.3 | convolution fusion | flops 43643904 | bytes 7202304 | tf_op jit(solution)/shard_map/dot_general | solution.py:46
  9.2 0.0 copy-done.4
  9.2 3.1 %abs_reduce_fusion.1 = (f32[3072]{0:T(1024)S(1)}, f32[384,3072]{1,0:T(8,128)}) fusion(f32[384]{0:T(512)S(1)} %copy-done.5, bf16[384,16]{0,1:T(8,128)(2,1)S(1)} %copy-done.7, bf16[16,3072]{1,0:T(8,128)(2,1)S(1)} %copy-done.4, bf16[384,3072]{1,0:T(8,128)(2,1)S(1)} %copy-done.2), kind=kOutput, calls=%fused_computation.5 | convolution fusion | flops 43643904 | bytes 7202304 | tf_op jit(solution)/shard_map/dot_general | solution.py:43
  12.3 0.6 broadcast_in_dim.2
  12.9 28.5 %all_to_all.63 = f32[32,1,9216]{2,1,0:T(1,128)S(1)} all-to-all(f32[32,1,9216]{2,1,0:T(1,128)S(1)} %broadcast_in_dim.2), channel_id=1, replica_groups=mesh['shard'=32,'model'=4] {'shard'}, dimensions={0} | all-to-all | bytes 2359296 | tf_op jit(solution)/shard_map/all_to_all | solution.py:11
  41.4 0.7 reduce_max.39
  42.0 2.8 %divide_convert_fusion.2 = bf16[384,3072]{1,0:T(8,128)(2,1)S(1)} fusion(f32[384,3072]{1,0:T(8,128)} %get-tuple-element.14, f32[3072]{0:T(1024)S(1)} %get-tuple-element.8), kind=kLoop, calls=%fused_computation.2 | loop fusion | flops 2359296 | bytes 7090176 | tf_op jit(solution)/shard_map/convert_element_type | solution.py:61
  44.9 2.4 %copy.35 = bf16[384,3072]{0,1:T(8,128)(2,1)} copy(bf16[384,3072]{1,0:T(8,128)(2,1)S(1)} %divide_convert_fusion.2) | data formatting | bytes 4718592 | tf_op jit(solution)/shard_map/convert_element_type | solution.py:61
  47.3 4.1 %all-to-all-start.1 = ((bf16[384,32,96]{0,2,1:T(8,128)(2,1)}), bf16[384,32,96]{0,2,1:T(8,128)(2,1)S(1)}, u32[]{:S(2)}, u32[]{:S(2)}) async-start(bf16[384,32,96]{0,2,1:T(8,128)(2,1)} %bitcast.20), calls=%async_computation.1 | async-start | bytes 4718592 | tf_op jit(solution)/shard_map/all_to_all | solution.py:66
  51.4 7.2 %divide_convert_fusion = (bf16[384,3072]{1,0:T(8,128)(2,1)}, bf16[384,3072]{1,0:T(8,128)(2,1)}) fusion(f32[384,3072]{1,0:T(8,128)} %get-tuple-element.10, f32[3072]{0:T(1024)S(1)} %get-tuple-element.6, f32[384,3072]{1,0:T(8,128)} %get-tuple-element.12, f32[3072]{0:T(1024)S(1)} %get-tuple-element.7), kind=kLoop, calls=%fused_computation | loop fusion | flops 4718592 | bytes 14180352 | tf_op jit(solution)/shard_map/convert_element_type | solution.py:63
  58.6 4.3 %copy.37 = bf16[384,3072]{0,1:T(8,128)(2,1)} copy(bf16[384,3072]{1,0:T(8,128)(2,1)} %get-tuple-element.16) | data formatting | bytes 4718592 | tf_op jit(solution)/shard_map/convert_element_type | solution.py:62
  62.9 20.1 %all-to-all-done.1 = bf16[384,32,96]{0,2,1:T(8,128)(2,1)S(1)} async-done(((bf16[384,32,96]{0,2,1:T(8,128)(2,1)}), bf16[384,32,96]{0,2,1:T(8,128)(2,1)S(1)}, u32[]{:S(2)}, u32[]{:S(2)}) %all-to-all-start.1) | async-done | bytes 2359328 | tf_op jit(solution)/shard_map/all_to_all | solution.py:66
  83.0 4.8 %all-to-all-start.2 = ((bf16[384,32,96]{0,2,1:T(8,128)(2,1)}), bf16[384,32,96]{0,2,1:T(8,128)(2,1)}, u32[]{:S(2)}, u32[]{:S(2)}) async-start(bf16[384,32,96]{0,2,1:T(8,128)(2,1)} %bitcast.21), calls=%async_computation.2 | async-start | bytes 4718592 | tf_op jit(solution)/shard_map/all_to_all | solution.py:67
  87.8 4.3 %copy.39 = bf16[384,3072]{0,1:T(8,128)(2,1)} copy(bf16[384,3072]{1,0:T(8,128)(2,1)} %get-tuple-element.15) | data formatting | bytes 4718592 | tf_op jit(solution)/shard_map/convert_element_type | solution.py:63
  92.0 25.5 %all-to-all-done.2 = bf16[384,32,96]{0,2,1:T(8,128)(2,1)} async-done(((bf16[384,32,96]{0,2,1:T(8,128)(2,1)}), bf16[384,32,96]{0,2,1:T(8,128)(2,1)}, u32[]{:S(2)}, u32[]{:S(2)}) %all-to-all-start.2) | async-done | bytes 2359328 | tf_op jit(solution)/shard_map/all_to_all | solution.py:67
  117.5 4.8 %all-to-all-start.3 = ((bf16[384,32,96]{0,2,1:T(8,128)(2,1)}), bf16[384,32,96]{0,2,1:T(8,128)(2,1)}, u32[]{:S(2)}, u32[]{:S(2)}) async-start(bf16[384,32,96]{0,2,1:T(8,128)(2,1)} %bitcast.19), calls=%async_computation.3 | async-start | bytes 4718592 | tf_op jit(solution)/shard_map/all_to_all | solution.py:68
  122.3 0.6 dynamic_slice.9
  122.9 0.6 dynamic_slice.10
  123.5 0.6 dynamic_slice.11
  124.1 1.7 %copy.45 = bf16[32,12,8,384]{3,2,0,1:T(8,128)(2,1)} copy(bf16[32,12,8,384]{3,2,1,0:T(8,128)(2,1)S(1)} %bitcast.18) | data formatting | bytes 4718592 | tf_op jit(solution)/shard_map/all_to_all | solution.py:66
  125.8 3.4 %copy.46 = bf16[32,12,8,384]{3,2,0,1:T(8,128)(2,1)} copy(bf16[32,12,8,384]{3,2,1,0:T(8,128)(2,1)} %bitcast.8) | data formatting | bytes 4718592 | tf_op jit(solution)/shard_map/all_to_all | solution.py:67
  129.2 23.3 %all-to-all-done.3 = bf16[384,32,96]{0,2,1:T(8,128)(2,1)} async-done(((bf16[384,32,96]{0,2,1:T(8,128)(2,1)}), bf16[384,32,96]{0,2,1:T(8,128)(2,1)}, u32[]{:S(2)}, u32[]{:S(2)}) %all-to-all-start.3) | async-done | bytes 2359328 | tf_op jit(solution)/shard_map/all_to_all | solution.py:68
  152.5 3.4 %copy.47 = bf16[32,12,8,384]{3,2,0,1:T(8,128)(2,1)} copy(bf16[32,12,8,384]{3,2,1,0:T(8,128)(2,1)} %bitcast.10) | data formatting | bytes 4718592 | tf_op jit(solution)/shard_map/all_to_all | solution.py:68
  (9 shorter events, 0.0 us)
Async XLA Ops:
  0.6 0.9 copy-start
  0.6 5.5 %copy-start.5 = (f32[384]{0:T(512)S(1)}, f32[384]{0:T(512)}, u32[]{:S(2)}) copy-start(f32[384]{0:T(512)} %param.19) | copy-start | bytes 4612
  0.7 5.5 %copy-start.6 = (bf16[384,16]{0,1:T(8,128)(2,1)S(1)}, bf16[384,16]{0,1:T(8,128)(2,1)}, u32[]{:S(2)}) copy-start(bf16[384,16]{0,1:T(8,128)(2,1)} %param.17) | copy-start | bytes 36868
  0.7 5.5 %copy-start.3 = (bf16[16,3072]{1,0:T(8,128)(2,1)S(1)}, bf16[16,3072]{1,0:T(8,128)(2,1)}, u32[]{:S(2)}) copy-start(bf16[16,3072]{1,0:T(8,128)(2,1)} %param.18) | copy-start | bytes 294916
  0.7 5.5 %copy-start.1 = (bf16[384,3072]{1,0:T(8,128)(2,1)S(1)}, bf16[384,3072]{1,0:T(8,128)(2,1)}, u32[]{:S(2)}) copy-start(bf16[384,3072]{1,0:T(8,128)(2,1)} %param.16) | copy-start | bytes 7077892
  6.2 3.0 %copy-start.2 = (bf16[384,3072]{1,0:T(8,128)(2,1)S(1)}, bf16[384,3072]{1,0:T(8,128)(2,1)}, u32[]{:S(2)}) copy-start(bf16[384,3072]{1,0:T(8,128)(2,1)} %param.13) | copy-start | bytes 7077892
  6.2 3.0 %copy-start.4 = (bf16[16,3072]{1,0:T(8,128)(2,1)S(1)}, bf16[16,3072]{1,0:T(8,128)(2,1)}, u32[]{:S(2)}) copy-start(bf16[16,3072]{1,0:T(8,128)(2,1)} %param.15) | copy-start | bytes 294916
  6.2 3.0 %copy-start.7 = (bf16[384,16]{0,1:T(8,128)(2,1)S(1)}, bf16[384,16]{0,1:T(8,128)(2,1)}, u32[]{:S(2)}) copy-start(bf16[384,16]{0,1:T(8,128)(2,1)} %param.14) | copy-start | bytes 36868
  47.3 35.6 %all-to-all-start.1 = ((bf16[384,32,96]{0,2,1:T(8,128)(2,1)}), bf16[384,32,96]{0,2,1:T(8,128)(2,1)S(1)}, u32[]{:S(2)}, u32[]{:S(2)}) async-start(bf16[384,32,96]{0,2,1:T(8,128)(2,1)} %bitcast.20), calls=%async_computation.1 | async-start | bytes 4718592 | tf_op jit(solution)/shard_map/all_to_all | solution.py:66
  83.0 34.6 %all-to-all-start.2 = ((bf16[384,32,96]{0,2,1:T(8,128)(2,1)}), bf16[384,32,96]{0,2,1:T(8,128)(2,1)}, u32[]{:S(2)}, u32[]{:S(2)}) async-start(bf16[384,32,96]{0,2,1:T(8,128)(2,1)} %bitcast.21), calls=%async_computation.2 | async-start | bytes 4718592 | tf_op jit(solution)/shard_map/all_to_all | solution.py:67
  117.5 34.9 %all-to-all-start.3 = ((bf16[384,32,96]{0,2,1:T(8,128)(2,1)}), bf16[384,32,96]{0,2,1:T(8,128)(2,1)}, u32[]{:S(2)}, u32[]{:S(2)}) async-start(bf16[384,32,96]{0,2,1:T(8,128)(2,1)} %bitcast.19), calls=%async_computation.3 | async-start | bytes 4718592 | tf_op jit(solution)/shard_map/all_to_all | solution.py:68
where the time goes:
time: 157 us; the launch traced here: 156 us
  waiting for transfers between devices  68.8 us (44%)
  blocking collectives  28.5 us (18%)
  local copies, waits for them, and re-layouts  22.7 us (14%)
  starting transfers between devices  13.7 us (9%)
  matrix products  10.7 us (7%)
  other arithmetic  10.7 us (7%)
    all_to_all x1, blocking collectives, sent_to_all(): return lax.all_to_all(copies, axis, split_axis=0, concat_axis=0, tiled=True)  28.5 us
    all_to_all x1, waiting for transfers between devices, on_device(): lax.all_to_all(narrow_key, 'shard', split_axis=1, concat_axis=0, tiled=True)  25.5 us
    all_to_all x1, waiting for transfers between devices, on_device(): lax.all_to_all(narrow_value, 'shard', split_axis=1, concat_axis=0, tiled=...  23.3 us
    all_to_all x1, waiting for transfers between devices, on_device(): lax.all_to_all(narrow_query, 'shard', split_axis=1, concat_axis=0, tiled=...  20.1 us
    convert_element_type x1, other arithmetic, on_device(): (result_gained_value / scale_value).astype(jnp.bfloat16)  7.22 us
    all_to_all x1, starting transfers between devices, on_device(): lax.all_to_all(narrow_value, 'shard', split_axis=1, concat_axis=0, tiled=...  4.8 us
    all_to_all x1, starting transfers between devices, on_device(): lax.all_to_all(narrow_key, 'shard', split_axis=1, concat_axis=0, tiled=True)  4.79 us
    dot_general x1, matrix products, on_device(): jnp.dot(low_query, high_query, preferred_element_type=jnp.float32)  4.65 us
  transfers between devices with their start and end apart: 3, of which 3 were waited for; matrix products, arithmetic and copies ran while one was open for 15% of the time, Pallas kernels for 0%

commit v1 on v0

v1 whole, which is shorter than its diff:
```python
import functools

import jax
import jax.numpy as jnp
from jax import lax
from jax.experimental import pallas as pl
from jax.experimental.pallas import tpu as pltpu
from jax.sharding import PartitionSpec as P

GROUP = 4
TAIL = 8
LANES = 128


def pack_kernel(*refs, cols, rank):
    ws, lows, gain, out = refs[:3], refs[3:6], refs[6], refs[7]
    inbox, lowbox, gbox, insem, lowsem = refs[8:]
    each = cols + rank
    wide = GROUP * cols
    groups = out.shape[0] // GROUP
    fetch = [
        [
            pltpu.make_async_copy(
                w.at[:, i * wide : (i + 1) * wide], inbox.at[m, i], insem.at[i, m]
            )
            for m, w in enumerate(ws)
        ]
        for i in range(groups)
    ]
    small = [
        pltpu.make_async_copy(low, lowbox.at[m], lowsem.at[m]) for m, low in enumerate(lows)
    ]
    small.append(pltpu.make_async_copy(gain, gbox, lowsem.at[3]))
    for copy in small:
        copy.start()
    for i in range(groups):
        for copy in fetch[i]:
            copy.start()
    for copy in small:
        copy.wait()
    g = gbox[...].reshape(1, -1)
    first = g.astype(jnp.bfloat16)
    rest = g - first.astype(jnp.float32)
    second = rest.astype(jnp.bfloat16)
    third = (rest - second.astype(jnp.float32)).astype(jnp.bfloat16)
    none = jnp.zeros((TAIL - 3, g.shape[1]), jnp.bfloat16)
    parts = jnp.concatenate([first, second, third, none], 0)
    for i in range(groups):
        for m in range(3):
            fetch[i][m].wait()
            turned = inbox[m, i].T
            for p in range(GROUP):
                at = i * GROUP + p
                out[at, m * each : m * each + cols, :] = turned[p * cols : (p + 1) * cols, :]
                out[at, m * each + cols : (m + 1) * each, :] = lowbox[m]
        for p in range(GROUP):
            out[i * GROUP + p, 3 * each :, :] = parts


def far(x):
    return pltpu.with_memory_space_constraint(x, pltpu.HBM)


def pack(weights, lows, gain, peers):
    rows, width = weights[0].shape
    rank = lows[0].shape[0]
    cols = width // peers
    tall = 3 * (cols + rank) + TAIL
    groups = peers // GROUP
    hbm = pl.BlockSpec(memory_space=pltpu.HBM)
    vmem = pl.BlockSpec(memory_space=pltpu.VMEM)
    return pl.pallas_call(
        functools.partial(pack_kernel, cols=cols, rank=rank),
        in_specs=[hbm] * 7,
        out_specs=vmem,
        out_shape=jax.ShapeDtypeStruct((peers, tall, rows), jnp.bfloat16),
        scratch_shapes=[
            pltpu.VMEM((3, groups, rows, GROUP * cols), jnp.bfloat16),
            pltpu.VMEM((3, rank, rows), jnp.bfloat16),
            pltpu.VMEM((rows,), jnp.float32),
            pltpu.SemaphoreType.DMA((groups, 3)),
            pltpu.SemaphoreType.DMA((4,)),
        ],
        compiler_params=pltpu.CompilerParams(vmem_limit_bytes=24 * 2**20),
        name="pack",
    )(*map(far, weights), *map(far, lows), far(gain))


def merge_kernel(got, *refs, cols):
    highs, finals, scales = refs[:3], refs[3:6], refs[6:9]
    highbox, wide, outbox, insem, outsem = refs[9:]
    rank, width = highs[0].shape
    each = cols + rank
    peers, tall, rows = got.shape
    start = lax.axis_index("shard") * cols
    base = jnp.minimum(start // LANES, width // LANES - 2) * LANES
    base = pl.multiple_of(base, LANES)
    fetch = [
        pltpu.make_async_copy(high.at[:, pl.ds(base, 2 * LANES)], highbox.at[m], insem.at[m])
        for m, high in enumerate(highs)
    ]
    for copy in fetch:
        copy.start()
    send = [
        [
            pltpu.make_async_copy(
                outbox.at[m, c * 32 : (c + 1) * 32], finals[m].at[c * 32 : (c + 1) * 32], outsem.at[m, c]
            )
            for c in range(cols // 32)
        ]
        for m in range(3)
    ]
    at_col = lax.broadcasted_iota(jnp.int32, (cols, 2 * LANES), 0) + (start - base)
    pick = (at_col == lax.broadcasted_iota(jnp.int32, (cols, 2 * LANES), 1)).astype(jnp.bfloat16)
    same = (
        lax.broadcasted_iota(jnp.int32, (cols, cols), 0)
        == lax.broadcasted_iota(jnp.int32, (cols, cols), 1)
    ).astype(jnp.bfloat16)
    for copy in fetch:
        copy.wait()
    for m in range(3):
        mine = lax.dot_general(
            pick, highbox[m], (((1,), (1,)), ((), ())), preferred_element_type=jnp.float32
        ).astype(jnp.bfloat16)
        mix = jnp.concatenate([same, mine], 1)
        top = jnp.zeros((cols, rows), jnp.float32)
        for p in range(peers):
            g = got[p, 3 * each : tall, :].astype(jnp.float32)
            gain = g[0:1, :] + g[1:2, :] + g[2:3, :]
            value = (
                jnp.dot(mix, got[p, m * each : (m + 1) * each, :], preferred_element_type=jnp.float32)
                * gain
            )
            wide[:, p * rows : (p + 1) * rows] = value
            top = jnp.maximum(top, jnp.abs(value))
        scale = jnp.max(top, axis=1, keepdims=True)
        scales[m][...] = jnp.broadcast_to(scale, (cols, LANES)).T[0:1, :]
        down = 1.0 / scale
        for c in range(cols // 32):
            part = slice(c * 32, (c + 1) * 32)
            for p in range(peers):
                at = slice(p * rows, (p + 1) * rows)
                outbox[m, part, at] = (wide[part, at] * down[part]).astype(jnp.bfloat16)
            send[m][c].start()
    for copies in send:
        for copy in copies:
            copy.wait()


def merge(got, highs, cols):
    peers, _, rows = got.shape
    rank = highs[0].shape[0]
    whole = jax.ShapeDtypeStruct((cols, peers * rows), jnp.bfloat16)
    line = jax.ShapeDtypeStruct((1, cols), jnp.float32)
    hbm = pl.BlockSpec(memory_space=pltpu.HBM)
    vmem = pl.BlockSpec(memory_space=pltpu.VMEM)
    return pl.pallas_call(
        functools.partial(merge_kernel, cols=cols),
        in_specs=[vmem] + [hbm] * 3,
        out_specs=[hbm] * 3 + [vmem] * 3,
        out_shape=[whole] * 3 + [line] * 3,
        scratch_shapes=[
            pltpu.VMEM((3, rank, 2 * LANES), jnp.bfloat16),
            pltpu.VMEM((cols, peers * rows), jnp.float32),
            pltpu.VMEM((3, cols, peers * rows), jnp.bfloat16),
            pltpu.SemaphoreType.DMA((3,)),
            pltpu.SemaphoreType.DMA((3, cols // 32)),
        ],
        compiler_params=pltpu.CompilerParams(vmem_limit_bytes=24 * 2**20),
        name="merge",
    )(got, *map(far, highs))


def on_device(
    w_query,
    low_query,
    high_query,
    w_key,
    low_key,
    high_key,
    w_value,
    low_value,
    high_value,
    norm_gain,
):
    peers = lax.axis_size("shard")
    cols = w_query.shape[1] // peers
    sent = pack(
        (w_query, w_key, w_value), (low_query.T, low_key.T, low_value.T), norm_gain, peers
    )
    got = lax.all_to_all(sent, "shard", split_axis=0, concat_axis=0, tiled=True)
    *finals, scale_query, scale_key, scale_value = merge(
        got, (high_query, high_key, high_value), cols
    )
    return (
        *(f.T for f in finals),
        scale_query.reshape(-1),
        scale_key.reshape(-1),
        scale_value.reshape(-1),
    )


def solution(mesh):
    return jax.shard_map(
        on_device,
        mesh=mesh,
        in_specs=(
            P("shard", "model"),
            P("shard", None),
            P(None, "model"),
            P("shard", "model"),
            P("shard", None),
            P(None, "model"),
            P("shard", "model"),
            P("shard", None),
            P(None, "model"),
            P("shard"),
        ),
        out_specs=(
            P(None, ("model", "shard")),
            P(None, ("model", "shard")),
            P(None, ("model", "shard")),
            P(("model", "shard")),
            P(("model", "shard")),
            P(("model", "shard")),
        ),
        check_vma=False,
    )
```

time: 157 us -> 121 us (0.77)
  blocking collectives: 28.5 us -> 106 us
  waiting for transfers between devices: 68.8 us -> 0 us
  local copies, waits for them, and re-layouts: 22.7 us -> 0 us
  starting transfers between devices: 13.7 us -> 0 us
  Pallas kernels: 0 us -> 13.3 us
  matrix products: 10.7 us -> 0 us
  other arithmetic: 10.7 us -> 0 us
    all_to_all x1, blocking collectives: 28.5 us -> 106 us  [on_device(): got = lax.all_to_all(sent, 'shard', split_axis=0, concat_axis=0, tiled=True)]
    all_to_all x3 -> x0, waiting for transfers between devices: 68.8 us -> none  [the longest x1 25.5 us: on_device(): lax.all_to_all(narrow_key, 'shard', split_axis=1, concat_axis=0, tiled=True)]
    all_to_all x3 -> x0, starting transfers between devices: 13.7 us -> none  [the longest x1 4.8 us: on_device(): lax.all_to_all(narrow_value, 'shard', split_axis=1, concat_axis=0, tiled=...]
    pallas_call x0 -> x2, Pallas kernels: none -> 13.3 us  [the longest x1 6.89 us: merge(): pl.pallas_call(functools.partial(merge_kernel, cols=cols), in_specs=[vmem...]
    convert_element_type x3 -> x0, local copies, waits for them, and re-layouts: 11 us -> none  [the longest x1 4.28 us: on_device(): (result_gained_key / scale_key).astype(jnp.bfloat16)]
    dot_general x3 -> x0, matrix products: 10.7 us -> none  [the longest x1 4.65 us: on_device(): jnp.dot(low_query, high_query, preferred_element_type=jnp.float32)]
    convert_element_type x2 -> x0, other arithmetic: 10 us -> none  [the longest x1 7.22 us: on_device(): (result_gained_value / scale_value).astype(jnp.bfloat16)]
    all_to_all x3 -> x0, local copies, waits for them, and re-layouts: 8.5 us -> none  [the longest x1 3.39 us: on_device(): lax.all_to_all(narrow_value, 'shard', split_axis=1, concat_axis=0, tiled=...]
  transfers between devices with their start and end apart: 3 -> 0, of which waited for: 3 -> 0; matrix products, arithmetic and copies ran while one was open for 15% -> 0% of each run, Pallas kernels for 0% -> 0%
where the time goes in v1:
time: 121 us; the launch traced here: 120 us
  blocking collectives  106 us (88%)
  Pallas kernels  13.3 us (11%)
    all_to_all x1, blocking collectives, on_device(): got = lax.all_to_all(sent, 'shard', split_axis=0, concat_axis=0, tiled=True)  106 us
    pallas_call x1, Pallas kernels, merge(): pl.pallas_call(functools.partial(merge_kernel, cols=cols), in_specs=[vmem...  6.89 us
    pallas_call x1, Pallas kernels, pack(): pl.pallas_call(functools.partial(pack_kernel, cols=cols, rank=rank), in_s...  6.43 us

profile of v1, /device:TPU:0, one launch (start us, length us, event | category | flops | bytes accessed | tf_op | source)
XLA Modules:
  0.0 120.4 jit_solution(11310487537565565621)
XLA Ops:
  0.6 6.4 %pack.1 = bf16[32,344,384]{2,1,0:T(8,128)(2,1)S(1)} custom-call(bf16[384,3072]{1,0:T(8,128)(2,1)} %refs_0_.2, bf16[384,3072]{1,0:T(8,128)(2,1)} %refs_1_.2, bf16[384,3072]{1,0:T(8,128)(2,1)} %refs_2_.2, bf16[16,384]{1,0:T(8,128)(2,1)} %bitcast.9, bf16[16,384]{1,0:T(8,128)(2,1)} %bitcast.10, bf16[16,384]{1,0:T(8,128)(2,1)} %bitcast.11, f32[384]{0:T(512)} %refs_6_.1), custom_call_target="tpu_custom_call" | custom-call | tf_op jit(solution)/shard_map/pack/pallas_call | solution.py:72
  7.1 106.4 %all_to_all.5.got = bf16[32,344,384]{2,1,0:T(8,128)(2,1)S(1)} all-to-all(bf16[32,344,384]{2,1,0:T(8,128)(2,1)S(1)} %pack.1), channel_id=1, replica_groups=mesh['shard'=32,'model'=4] {'shard'}, dimensions={0} | all-to-all | bytes 16908288 | tf_op jit(solution)/shard_map/all_to_all | solution.py:191
  113.5 6.9 %merge.1 = (bf16[96,12288]{1,0:T(8,128)(2,1)}, bf16[96,12288]{1,0:T(8,128)(2,1)}, bf16[96,12288]{1,0:T(8,128)(2,1)}, f32[1,96]{1,0:T(1,128)}, f32[1,96]{1,0:T(1,128)}, /*index=5*/f32[1,96]{1,0:T(1,128)}) custom-call(bf16[32,344,384]{2,1,0:T(8,128)(2,1)S(1)} %all_to_all.5.got, bf16[16,3072]{1,0:T(8,128)(2,1)} %refs_0_.3, bf16[16,3072]{1,0:T(8,128)(2,1)} %refs_1_.3, ...), custom_call_target="tpu_custom_call" | custom-call | tf_op jit(solution)/shard_map/merge/pallas_call | solution.py:157

commit v2 on v1

v2 whole, which is shorter than its diff:
```python
import functools

import jax
import jax.numpy as jnp
from jax import lax
from jax.experimental import pallas as pl
from jax.experimental.pallas import tpu as pltpu
from jax.sharding import PartitionSpec as P

GROUP = 4
TAIL = 8
LANES = 128


def split3(g):
    first = g.astype(jnp.bfloat16)
    rest = g - first.astype(jnp.float32)
    second = rest.astype(jnp.bfloat16)
    third = (rest - second.astype(jnp.float32)).astype(jnp.bfloat16)
    none = jnp.zeros((TAIL - 3, g.shape[1]), jnp.bfloat16)
    return jnp.concatenate([first, second, third, none], 0)


def pack_kernel(*refs, cols, rank):
    ws, lows, gain, highs, out, mix = refs[:3], refs[3:6], refs[6], refs[7:10], refs[10], refs[11]
    inbox, lowbox, gbox, highbox, insem, lowsem = refs[12:]
    each = cols + rank
    wide = GROUP * cols
    groups = out.shape[0] // GROUP
    width = ws[0].shape[1]
    start = lax.axis_index("shard") * cols
    base = jnp.minimum(start // LANES, width // LANES - 2) * LANES
    base = pl.multiple_of(base, LANES)
    fetch = [
        [
            pltpu.make_async_copy(
                w.at[:, i * wide : (i + 1) * wide], inbox.at[m, i], insem.at[i, m]
            )
            for m, w in enumerate(ws)
        ]
        for i in range(groups)
    ]
    small = [
        pltpu.make_async_copy(low, lowbox.at[m], lowsem.at[m]) for m, low in enumerate(lows)
    ]
    small += [
        pltpu.make_async_copy(high.at[:, pl.ds(base, 2 * LANES)], highbox.at[m], lowsem.at[3 + m])
        for m, high in enumerate(highs)
    ]
    small.append(pltpu.make_async_copy(gain, gbox, lowsem.at[6]))
    for i in range(groups):
        for copy in fetch[i]:
            copy.start()
        if i == 1:
            for copy in small:
                copy.start()
    for i in range(groups):
        for m in range(3):
            fetch[i][m].wait()
            turned = inbox[m, i].T
            for p in range(GROUP):
                at = i * GROUP + p
                out[at, m * each : m * each + cols, :] = turned[p * cols : (p + 1) * cols, :]
        if i == 2:
            for copy in small:
                copy.wait()
            parts = split3(gbox[...].reshape(1, -1))
            at_col = lax.broadcasted_iota(jnp.int32, (cols, 2 * LANES), 0) + (start - base)
            pick = at_col == lax.broadcasted_iota(jnp.int32, (cols, 2 * LANES), 1)
            pick = pick.astype(jnp.bfloat16)
            same = (
                lax.broadcasted_iota(jnp.int32, (cols, cols), 0)
                == lax.broadcasted_iota(jnp.int32, (cols, cols), 1)
            ).astype(jnp.bfloat16)
            for m in range(3):
                mine = lax.dot_general(
                    pick, highbox[m], (((1,), (1,)), ((), ())), preferred_element_type=jnp.float32
                )
                mix[m] = jnp.concatenate([same, mine.astype(jnp.bfloat16)], 1)
        if i == 3:
            for at in range(groups * GROUP):
                for m in range(3):
                    out[at, m * each + cols : (m + 1) * each, :] = lowbox[m]
                out[at, 3 * each :, :] = parts


def far(x):
    return pltpu.with_memory_space_constraint(x, pltpu.HBM)


def pack(weights, lows, gain, highs, peers):
    rows, width = weights[0].shape
    rank = lows[0].shape[0]
    cols = width // peers
    tall = 3 * (cols + rank) + TAIL
    groups = peers // GROUP
    hbm = pl.BlockSpec(memory_space=pltpu.HBM)
    vmem = pl.BlockSpec(memory_space=pltpu.VMEM)
    return pl.pallas_call(
        functools.partial(pack_kernel, cols=cols, rank=rank),
        in_specs=[hbm] * 10,
        out_specs=[vmem] * 2,
        out_shape=[
            jax.ShapeDtypeStruct((peers, tall, rows), jnp.bfloat16),
            jax.ShapeDtypeStruct((3, cols, cols + rank), jnp.bfloat16),
        ],
        scratch_shapes=[
            pltpu.VMEM((3, groups, rows, GROUP * cols), jnp.bfloat16),
            pltpu.VMEM((3, rank, rows), jnp.bfloat16),
            pltpu.VMEM((rows,), jnp.float32),
            pltpu.VMEM((3, rank, 2 * LANES), jnp.bfloat16),
            pltpu.SemaphoreType.DMA((groups, 3)),
            pltpu.SemaphoreType.DMA((7,)),
        ],
        compiler_params=pltpu.CompilerParams(vmem_limit_bytes=24 * 2**20),
        name="pack",
    )(*map(far, weights), *map(far, lows), far(gain), *map(far, highs))


def merge_kernel(got, mix, *refs):
    finals, scales = refs[:3], refs[3:6]
    wide, outbox, outsem = refs[6:]
    _, cols, each = mix.shape
    peers, tall, rows = got.shape
    send = [
        [
            pltpu.make_async_copy(
                outbox.at[m, c * 32 : (c + 1) * 32], finals[m].at[c * 32 : (c + 1) * 32], outsem.at[m, c]
            )
            for c in range(cols // 32)
        ]
        for m in range(3)
    ]
    for m in range(3):
        top = jnp.zeros((cols, rows), jnp.float32)
        for p in range(peers):
            g = got[p, 3 * each : tall, :].astype(jnp.float32)
            gain = g[0:1, :] + g[1:2, :] + g[2:3, :]
            value = (
                jnp.dot(mix[m], got[p, m * each : (m + 1) * each, :], preferred_element_type=jnp.float32)
                * gain
            )
            wide[:, p * rows : (p + 1) * rows] = value
            top = jnp.maximum(top, jnp.abs(value))
        scale = jnp.max(top, axis=1, keepdims=True)
        scales[m][...] = jnp.broadcast_to(scale, (cols, LANES)).T[0:1, :]
        down = 1.0 / scale
        for c in range(cols // 32):
            part = slice(c * 32, (c + 1) * 32)
            for p in range(peers):
                at = slice(p * rows, (p + 1) * rows)
                outbox[m, part, at] = (wide[part, at] * down[part]).astype(jnp.bfloat16)
            send[m][c].start()
    for copies in send:
        for copy in copies:
            copy.wait()


def merge(got, mix):
    peers, _, rows = got.shape
    _, cols, _ = mix.shape
    whole = jax.ShapeDtypeStruct((cols, peers * rows), jnp.bfloat16)
    line = jax.ShapeDtypeStruct((1, cols), jnp.float32)
    hbm = pl.BlockSpec(memory_space=pltpu.HBM)
    vmem = pl.BlockSpec(memory_space=pltpu.VMEM)
    return pl.pallas_call(
        merge_kernel,
        in_specs=[vmem] * 2,
        out_specs=[hbm] * 3 + [vmem] * 3,
        out_shape=[whole] * 3 + [line] * 3,
        scratch_shapes=[
            pltpu.VMEM((cols, peers * rows), jnp.float32),
            pltpu.VMEM((3, cols, peers * rows), jnp.bfloat16),
            pltpu.SemaphoreType.DMA((3, cols // 32)),
        ],
        compiler_params=pltpu.CompilerParams(vmem_limit_bytes=24 * 2**20),
        name="merge",
    )(got, mix)


def on_device(
    w_query,
    low_query,
    high_query,
    w_key,
    low_key,
    high_key,
    w_value,
    low_value,
    high_value,
    norm_gain,
):
    sent, mix = pack(
        (w_query, w_key, w_value),
        (low_query.T, low_key.T, low_value.T),
        norm_gain,
        (high_query, high_key, high_value),
        lax.axis_size("shard"),
    )
    got = lax.all_to_all(sent, "shard", split_axis=0, concat_axis=0, tiled=True)
    *finals, scale_query, scale_key, scale_value = merge(got, mix)
    return (
        *(f.T for f in finals),
        scale_query.reshape(-1),
        scale_key.reshape(-1),
        scale_value.reshape(-1),
    )


def solution(mesh):
    return jax.shard_map(
        on_device,
        mesh=mesh,
        in_specs=(
            P("shard", "model"),
            P("shard", None),
            P(None, "model"),
            P("shard", "model"),
            P("shard", None),
            P(None, "model"),
            P("shard", "model"),
            P("shard", None),
            P(None, "model"),
            P("shard"),
        ),
        out_specs=(
            P(None, ("model", "shard")),
            P(None, ("model", "shard")),
            P(None, ("model", "shard")),
            P(("model", "shard")),
            P(("model", "shard")),
            P(("model", "shard")),
        ),
        check_vma=False,
    )
```

time: 121 us -> 119 us (0.983)
  Pallas kernels: 13.3 us -> 11.4 us
where the time goes in v2:
time: 119 us; the launch traced here: 118 us
  blocking collectives  106 us (89%)
  Pallas kernels  11.4 us (10%)
    all_to_all x1, blocking collectives, on_device(): got = lax.all_to_all(sent, 'shard', split_axis=0, concat_axis=0, tiled=True)  106 us
    pallas_call x1, Pallas kernels, merge(): pl.pallas_call(merge_kernel, in_specs=[vmem] * 2, out_specs=[hbm] * 3 + [...  5.89 us
    pallas_call x1, Pallas kernels, pack(): pl.pallas_call(functools.partial(pack_kernel, cols=cols, rank=rank), in_s...  5.48 us

profile of v2, /device:TPU:0, one launch (start us, length us, event | category | flops | bytes accessed | tf_op | source)
XLA Modules:
  0.0 118.4 jit_solution(14101517624321898150)
XLA Ops:
  0.6 5.5 %pack.1 = (bf16[32,344,384]{2,1,0:T(8,128)(2,1)S(1)}, bf16[3,96,112]{2,1,0:T(8,128)(2,1)S(1)}) custom-call(bf16[384,3072]{1,0:T(8,128)(2,1)} %refs_0_.1, bf16[384,3072]{1,0:T(8,128)(2,1)} %refs_1_.1, bf16[384,3072]{1,0:T(8,128)(2,1)} %refs_2_.1, bf16[16,384]{1,0:T(8,128)(2,1)} %bitcast.9, bf16[16,384]{1,0:T(8,128)(2,1)} %bitcast.10, ...), custom_call_target="tpu_custom_call" | custom-call | tf_op jit(solution)/shard_map/pack/pallas_call | solution.py:99
  6.1 106.4 %all_to_all.5.got = bf16[32,344,384]{2,1,0:T(8,128)(2,1)S(1)} all-to-all(bf16[32,344,384]{2,1,0:T(8,128)(2,1)S(1)} %get-tuple-element.14), channel_id=1, replica_groups=mesh['shard'=32,'model'=4] {'shard'}, dimensions={0} | all-to-all | bytes 16908288 | tf_op jit(solution)/shard_map/all_to_all | solution.py:200
  112.6 5.9 %merge.1 = (bf16[96,12288]{1,0:T(8,128)(2,1)}, bf16[96,12288]{1,0:T(8,128)(2,1)}, bf16[96,12288]{1,0:T(8,128)(2,1)}, f32[1,96]{1,0:T(1,128)}, f32[1,96]{1,0:T(1,128)}, /*index=5*/f32[1,96]{1,0:T(1,128)}) custom-call(bf16[32,344,384]{2,1,0:T(8,128)(2,1)S(1)} %all_to_all.5.got, bf16[3,96,112]{2,1,0:T(8,128)(2,1)S(1)} %get-tuple-element.15.mix), custom_call_target="tpu_custom_call" | custom-call | tf_op jit(solution)/shard_map/merge/pallas_call | solution.py:166

commit v3 on v0

v3 whole, which is shorter than its diff:
```python
import functools

import jax
import jax.numpy as jnp
from jax import lax
from jax.experimental import pallas as pl
from jax.experimental.pallas import tpu as pltpu
from jax.sharding import PartitionSpec as P


SIDE = 4
PLANE = 8
PEERS = SIDE * PLANE
GROUP = 4
LANES = 128
EARLY = 32
TAIL = 8
HBM = pl.BlockSpec(memory_space=pltpu.HBM)
VMEM = pl.BlockSpec(memory_space=pltpu.VMEM)
PARAMS = pltpu.CompilerParams(vmem_limit_bytes=30 * 2**20)


def moved(place, dz, i):
    dy, dx = i // 2, i % 2
    z, y, x = place // PLANE, (place // 2) % SIDE, place % 2
    return ((z + dz) % SIDE) * PLANE + ((y + dy) % SIDE) * 2 + (x + dx) % 2


def came_from(place, dz, i):
    return moved(place, -dz % SIDE, (-(i // 2) % SIDE) * 2 + i % 2)


def far(x):
    return pltpu.with_memory_space_constraint(x, pltpu.HBM)


def shape(*dims):
    return jax.ShapeDtypeStruct(dims, jnp.bfloat16)


def split3(g):
    first = g.astype(jnp.bfloat16)
    rest = g - first.astype(jnp.float32)
    second = rest.astype(jnp.bfloat16)
    third = (rest - second.astype(jnp.float32)).astype(jnp.bfloat16)
    none = jnp.zeros((TAIL - 3, g.shape[1]), jnp.bfloat16)
    return jnp.concatenate([first, second, third, none], 0)


def fetches(ws, inbox, insem):
    groups = PEERS // GROUP
    wide = ws[0].shape[1] // groups
    return [
        [
            pltpu.make_async_copy(
                w.at[:, i * wide : (i + 1) * wide], inbox.at[m, i], insem.at[i, m]
            )
            for m, w in enumerate(ws)
        ]
        for i in range(groups)
    ]


def turn_group(i, fetch, inbox, turn, cols):
    for m, copy in enumerate(fetch[i]):
        copy.wait()
        turned = inbox[m, i].T
        for p in range(GROUP):
            turn[i * GROUP + p, m * cols : (m + 1) * cols, :] = turned[p * cols : (p + 1) * cols, :]


def pack_ac_kernel(wq, wk, low, *refs, cols):
    lot_a, lot_c = refs[:SIDE], refs[SIDE : SIDE + PLANE]
    inbox, turn, lowbox, insem, lowsem = refs[SIDE + PLANE :]
    first = cols + EARLY
    rest = cols - EARLY
    place = lax.axis_index("shard")
    small = pltpu.make_async_copy(low, lowbox, lowsem)
    fetch = fetches((wq, wk), inbox, insem)
    for copies in fetch:
        for copy in copies:
            copy.start()
    small.start()
    for i in range(PEERS // GROUP):
        turn_group(i, fetch, inbox, turn, cols)
    small.wait()
    for dz in range(SIDE):
        lot_a[dz][PLANE * first :, :] = lowbox[...]
        for i in range(PLANE):
            to = moved(place, dz, i)
            lot_a[dz][i * first : (i + 1) * first, :] = turn[to, 0:first, :]
            lot_c[i][dz * rest : (dz + 1) * rest, :] = turn[to, first:, :]


def pack_ac(w_query, w_key, low):
    rows, width = w_query.shape
    rank = low.shape[0]
    cols = width // PEERS
    groups = PEERS // GROUP
    out = [shape(PLANE * (cols + EARLY) + rank, rows)] * SIDE
    out += [shape(SIDE * (cols - EARLY), rows)] * PLANE
    got = pl.pallas_call(
        functools.partial(pack_ac_kernel, cols=cols),
        in_specs=[HBM] * 3,
        out_specs=[VMEM] * len(out),
        out_shape=out,
        scratch_shapes=[
            pltpu.VMEM((2, groups, rows, GROUP * cols), jnp.bfloat16),
            pltpu.VMEM((PEERS, 2 * cols, rows), jnp.bfloat16),
            pltpu.VMEM((rank, rows), jnp.bfloat16),
            pltpu.SemaphoreType.DMA((groups, 2)),
            pltpu.SemaphoreType.DMA,
        ],
        compiler_params=PARAMS,
        name="pack_ac",
    )(far(w_query), far(w_key), far(low))
    return got[:SIDE], got[SIDE:]


def pack_b_kernel(wv, low_k, low_v, gain, *refs, cols):
    highs, lot, mix = refs[:3], refs[3 : 3 + PLANE], refs[3 + PLANE]
    inbox, turn, lowbox, gbox, highbox, insem, lowsem = refs[4 + PLANE :]
    width = wv.shape[1]
    place = lax.axis_index("shard")
    core = lax.axis_index("model") % 2
    start = place * cols
    base = jnp.minimum(start // LANES, width // LANES - 2) * LANES
    base = pl.multiple_of(base, LANES)
    fetch = fetches((wv,), inbox, insem)
    for copies in fetch:
        copies[0].start()
    small = [
        pltpu.make_async_copy(high.at[:, pl.ds(base, 2 * LANES)], highbox.at[m], lowsem.at[m])
        for m, high in enumerate(highs)
    ]
    small.append(pltpu.make_async_copy(gain, gbox, lowsem.at[3]))
    for copy in small:
        copy.start()
    even = pltpu.make_async_copy(low_k, lowbox, lowsem.at[4])
    odd = pltpu.make_async_copy(low_v, lowbox, lowsem.at[4])

    @pl.when(core == 0)
    def _():
        even.start()

    @pl.when(core == 1)
    def _():
        odd.start()

    for i in range(PEERS // GROUP):
        turn_group(i, fetch, inbox, turn, cols)
    for copy in (*small, even):
        copy.wait()
    at_col = lax.broadcasted_iota(jnp.int32, (cols, 2 * LANES), 0) + (start - base)
    pick = at_col == lax.broadcasted_iota(jnp.int32, (cols, 2 * LANES), 1)
    pick = pick.astype(jnp.bfloat16)
    same = (
        lax.broadcasted_iota(jnp.int32, (cols, cols), 0)
        == lax.broadcasted_iota(jnp.int32, (cols, cols), 1)
    ).astype(jnp.bfloat16)
    for m in range(3):
        own = lax.dot_general(
            pick, highbox[m], (((1,), (1,)), ((), ())), preferred_element_type=jnp.float32
        )
        mix[m] = jnp.concatenate([same, own.astype(jnp.bfloat16)], 1)
    parts = split3(gbox[...].reshape(1, -1))
    rank = lowbox.shape[0]
    for i in range(PLANE):
        for dz in range(SIDE):
            lot[i][dz * cols : (dz + 1) * cols, :] = turn[moved(place, dz, i)]
        lot[i][SIDE * cols : SIDE * cols + rank, :] = lowbox[...]
        lot[i][SIDE * cols + rank :, :] = parts


def pack_b(w_value, low_key, low_value, gain, highs):
    rows, width = w_value.shape
    rank = low_key.shape[0]
    cols = width // PEERS
    groups = PEERS // GROUP
    out = [shape(SIDE * cols + rank + TAIL, rows)] * PLANE + [shape(3, cols, cols + rank)]
    *lot, mix = pl.pallas_call(
        functools.partial(pack_b_kernel, cols=cols),
        in_specs=[HBM] * 7,
        out_specs=[VMEM] * len(out),
        out_shape=out,
        scratch_shapes=[
            pltpu.VMEM((1, groups, rows, GROUP * cols), jnp.bfloat16),
            pltpu.VMEM((PEERS, cols, rows), jnp.bfloat16),
            pltpu.VMEM((rank, rows), jnp.bfloat16),
            pltpu.VMEM((rows,), jnp.float32),
            pltpu.VMEM((3, rank, 2 * LANES), jnp.bfloat16),
            pltpu.SemaphoreType.DMA((groups, 1)),
            pltpu.SemaphoreType.DMA((5,)),
        ],
        compiler_params=PARAMS,
        name="pack_b",
    )(far(w_value), far(low_key), far(low_value), far(gain), *map(far, highs))
    return lot, mix


def repack(parts, moves, tall, count):
    def kernel(*refs):
        ins, outs = refs[: len(parts)], refs[len(parts) :]
        for k, to, j, at, n in moves:
            outs[k][to : to + n, :] = ins[j][at : at + n, :]

    out = [shape(tall, parts[0].shape[1])] * count
    return pl.pallas_call(
        kernel,
        in_specs=[VMEM] * len(parts),
        out_specs=[VMEM] * count,
        out_shape=out,
        compiler_params=PARAMS,
    )(*parts)


def place_all():
    return [(dz, i) for dz in range(SIDE) for i in range(PLANE)]


def finish(m, value_of, mix, scale_ref, wide, outbox, final, outsem):
    _, cols, _ = mix.shape
    rows = wide.shape[2]
    place = lax.axis_index("shard")
    top = jnp.zeros((cols, rows), jnp.float32)
    for dz, i in place_all():
        packed, g = value_of(dz, i)
        g = g.astype(jnp.float32)
        gain = g[0:1, :] + g[1:2, :] + g[2:3, :]
        value = jnp.dot(mix[m], packed, preferred_element_type=jnp.float32) * gain
        wide[came_from(place, dz, i)] = value
        top = jnp.maximum(top, jnp.abs(value))
    scale = jnp.max(top, axis=1, keepdims=True)
    scale_ref[...] = jnp.broadcast_to(scale, (cols, LANES)).T[0:1, :]
    down = 1.0 / scale
    copies = []
    for c in range(cols // 32):
        part = slice(c * 32, (c + 1) * 32)
        for p in range(PEERS):
            outbox[part, p * rows : (p + 1) * rows] = (wide[p, part] * down[part]).astype(
                jnp.bfloat16
            )
        copies.append(pltpu.make_async_copy(outbox.at[part], final.at[part], outsem.at[c]))
        copies[-1].start()
    return copies


def merge_v_kernel(*refs):
    lot, theirs, mix, final, scale = refs[:SIDE], *refs[SIDE : SIDE + 4]
    wide, outbox, outsem = refs[SIDE + 4 :]
    _, cols, each = mix.shape
    rank = each - cols
    block = each + TAIL
    mine_is_value = lax.axis_index("model") % 2 == 1

    def value_of(dz, i):
        at = i * block
        other = (dz * PLANE + i) * (rank + TAIL)
        own = lot[dz][at + cols : at + each, :]
        low = jnp.where(mine_is_value, own, theirs[other : other + rank, :])
        packed = jnp.concatenate([lot[dz][at : at + cols, :], low], 0)
        return packed, lot[dz][at + each : at + block, :]

    for copy in finish(2, value_of, mix, scale, wide, outbox, final, outsem):
        copy.wait()


def merge_qk_kernel(*refs):
    lot_a, lot_c = refs[:PLANE], refs[PLANE : PLANE + SIDE]
    mine, theirs, mix, final_q, final_k, scale_q, scale_k = refs[PLANE + SIDE : PLANE + SIDE + 7]
    wide, outbox, outsem = refs[PLANE + SIDE + 7 :]
    _, cols, each = mix.shape
    rank = each - cols
    block = each + EARLY
    rest = cols - EARLY
    mine_is_key = lax.axis_index("model") % 2 == 0

    def gain_of(dz, i):
        at = (dz * PLANE + i) * (rank + TAIL)
        return mine[at + rank : at + rank + TAIL, :]

    def query_of(dz, i):
        return lot_a[i][dz * block : dz * block + each, :], gain_of(dz, i)

    def key_of(dz, i):
        at = (dz * PLANE + i) * (rank + TAIL)
        low = jnp.where(mine_is_key, mine[at : at + rank, :], theirs[at : at + rank, :])
        early = lot_a[i][dz * block + each : (dz + 1) * block, :]
        late = lot_c[dz][i * rest : (i + 1) * rest, :]
        return jnp.concatenate([early, late, low], 0), gain_of(dz, i)

    copies = finish(0, query_of, mix, scale_q, wide, outbox.at[0], final_q, outsem.at[0])
    copies += finish(1, key_of, mix, scale_k, wide, outbox.at[1], final_k, outsem.at[1])
    for copy in copies:
        copy.wait()


def merge(kernel, operands, mix, rows, count):
    _, cols, _ = mix.shape
    lead = () if count == 1 else (count,)
    return pl.pallas_call(
        kernel,
        in_specs=[VMEM] * (len(operands) + 1),
        out_specs=[HBM] * count + [VMEM] * count,
        out_shape=[shape(cols, PEERS * rows)] * count
        + [jax.ShapeDtypeStruct((1, cols), jnp.float32)] * count,
        scratch_shapes=[
            pltpu.VMEM((PEERS, cols, rows), jnp.float32),
            pltpu.VMEM((*lead, cols, PEERS * rows), jnp.bfloat16),
            pltpu.SemaphoreType.DMA((*lead, cols // 32)),
        ],
        compiler_params=PARAMS,
    )(*operands, mix)


def on_device(
    w_query,
    low_query,
    high_query,
    w_key,
    low_key,
    high_key,
    w_value,
    low_value,
    high_value,
    norm_gain,
):
    rows = w_query.shape[0]
    cols = w_query.shape[1] // PEERS
    rank = low_query.shape[1]
    each = cols + rank
    first, rest = cols + EARLY, cols - EARLY
    extra = rank + TAIL
    models = lax.axis_size("model")

    def leg(part, dz, i):
        pairs = [(s, moved(s, dz, i)) for s in range(PEERS)]
        return lax.ppermute(part, "shard", pairs)

    def along_z(lot):
        return [lot[0], *(leg(lot[dz], dz, 0) for dz in range(1, SIDE))]

    def in_plane(lot):
        return [lot[0], *(leg(lot[i], 0, i) for i in range(1, PLANE))]

    lot_a, lot_c = pack_ac(w_query, w_key, low_query.T)
    lot_b, mix = pack_b(
        w_value, low_key.T, low_value.T, norm_gain, (high_query, high_key, high_value)
    )
    lot_a = along_z(lot_a)
    lot_b = in_plane(lot_b)
    lot_c = in_plane(lot_c)
    moves = []
    for dz, i in place_all():
        moves.append((dz, i * (cols + extra), i, dz * cols, cols))
        moves.append((dz, i * (cols + extra) + cols, i, SIDE * cols, extra))
    lot_b = repack(lot_b, moves, PLANE * (cols + extra), SIDE)
    lot_b = along_z(lot_b)
    moves = []
    for dz, i in place_all():
        to = dz * (each + EARLY)
        moves.append((i, to, dz, i * first, cols))
        moves.append((i, to + cols, dz, PLANE * first, rank))
        moves.append((i, to + each, dz, i * first + cols, EARLY))
    lot_a = repack(lot_a, moves, SIDE * (each + EARLY), PLANE)
    lot_a = in_plane(lot_a)
    moves = [(dz, i * rest, i, dz * rest, rest) for dz, i in place_all()]
    lot_c = repack(lot_c, moves, PLANE * rest, SIDE)
    lot_c = along_z(lot_c)
    moves = [
        (0, (dz * PLANE + i) * extra, dz, i * (cols + extra) + cols, extra)
        for dz, i in place_all()
    ]
    (mine,) = repack(lot_b, moves, PEERS * extra, 1)
    theirs = lax.ppermute(mine, "model", [(m, m ^ 1) for m in range(models)])
    final_v, scale_v = merge(merge_v_kernel, (*lot_b, theirs), mix, rows, 1)
    final_q, final_k, scale_q, scale_k = merge(
        merge_qk_kernel, (*lot_a, *lot_c, mine, theirs), mix, rows, 2
    )
    return (
        final_q.T,
        final_k.T,
        final_v.T,
        scale_q.reshape(-1),
        scale_k.reshape(-1),
        scale_v.reshape(-1),
    )


def solution(mesh):
    return jax.shard_map(
        on_device,
        mesh=mesh,
        in_specs=(
            P("shard", "model"),
            P("shard", None),
            P(None, "model"),
            P("shard", "model"),
            P("shard", None),
            P(None, "model"),
            P("shard", "model"),
            P("shard", None),
            P(None, "model"),
            P("shard"),
        ),
        out_specs=(
            P(None, ("model", "shard")),
            P(None, ("model", "shard")),
            P(None, ("model", "shard")),
            P(("model", "shard")),
            P(("model", "shard")),
            P(("model", "shard")),
        ),
        check_vma=False,
    )
```

time: 157 us -> 180 us (1.15)
  starting transfers between devices: 13.7 us -> 89.3 us
  blocking collectives: 28.5 us -> 0 us
  local copies, waits for them, and re-layouts: 22.7 us -> 0 us
  Pallas kernels: 0 us -> 14.4 us
  matrix products: 10.7 us -> 0 us
  other arithmetic: 10.7 us -> 0 us
  waiting for transfers between devices: 68.8 us -> 73.9 us
    ppermute x0 -> x31, starting transfers between devices: none -> 89.3 us  [the longest x30 89.2 us: leg(): return lax.ppermute(part, 'shard', pairs)]
    ppermute x0 -> x31, waiting for transfers between devices: none -> 73.9 us  [the longest x30 73.9 us: leg(): return lax.ppermute(part, 'shard', pairs)]
    all_to_all x3 -> x0, waiting for transfers between devices: 68.8 us -> none  [the longest x1 25.5 us: on_device(): lax.all_to_all(narrow_key, 'shard', split_axis=1, concat_axis=0, tiled=True)]
    all_to_all x1 -> x0, blocking collectives: 28.5 us -> none  [sent_to_all(): return lax.all_to_all(copies, axis, split_axis=0, concat_axis=0, tiled=True)]
    pallas_call x0 -> x8, Pallas kernels: none -> 14.4 us  [the longest x2 7.19 us: merge(): pl.pallas_call(kernel, in_specs=[VMEM] * (len(operands) + 1), out_specs=[...]
    all_to_all x3 -> x0, starting transfers between devices: 13.7 us -> none  [the longest x1 4.8 us: on_device(): lax.all_to_all(narrow_value, 'shard', split_axis=1, concat_axis=0, tiled=...]
    convert_element_type x3 -> x0, local copies, waits for them, and re-layouts: 11 us -> none  [the longest x1 4.28 us: on_device(): (result_gained_key / scale_key).astype(jnp.bfloat16)]
    dot_general x3 -> x0, matrix products: 10.7 us -> none  [the longest x1 4.65 us: on_device(): jnp.dot(low_query, high_query, preferred_element_type=jnp.float32)]
  transfers between devices with their start and end apart: 3 -> 31, of which waited for: 3 -> 13; matrix products, arithmetic and copies ran while one was open for 15% -> 0% of each run, Pallas kernels for 0% -> 4%
where the time goes in v3:
time: 180 us; the launch traced here: 178 us
  starting transfers between devices  89.3 us (50%)
  waiting for transfers between devices  73.9 us (41%)
  Pallas kernels  14.4 us (8%)
    ppermute x30, starting transfers between devices, leg(): return lax.ppermute(part, 'shard', pairs)  89.2 us
    ppermute x30, waiting for transfers between devices, leg(): return lax.ppermute(part, 'shard', pairs)  73.9 us
    pallas_call x2, Pallas kernels, merge(): pl.pallas_call(kernel, in_specs=[VMEM] * (len(operands) + 1), out_specs=[...  7.19 us
    pallas_call x1, Pallas kernels, pack_ac(): pl.pallas_call(functools.partial(pack_ac_kernel, cols=cols), in_specs=[HB...  3.78 us
  transfers between devices with their start and end apart: 31, of which 13 were waited for; matrix products, arithmetic and copies ran while one was open for 0% of the time, Pallas kernels for 4%

profile of v3, /device:TPU:0, one launch (start us, length us, event | category | flops | bytes accessed | tf_op | source)
XLA Modules:
  0.0 178.5 jit_solution(5298585588142086955)
XLA Ops:
  0.6 2.7 %pack_b.1 = (bf16[408,384]{1,0:T(8,128)(2,1)S(1)}, bf16[408,384]{1,0:T(8,128)(2,1)S(1)}, bf16[408,384]{1,0:T(8,128)(2,1)S(1)}, bf16[408,384]{1,0:T(8,128)(2,1)S(...) custom-call(bf16[384,3072]{1,0:T(8,128)(2,1)} %wv.1, ...), custom_call_target="tpu_custom_call" | custom-call | tf_op jit(solution)/shard_map/pack_b/pallas_call | solution.py:181
  3.3 1.7 collective-permute-start.20
  9.6 3.0 %collective-permute-start.24 = (bf16[408,384]{1,0:T(8,128)(2,1)S(1)}, bf16[408,384]{1,0:T(8,128)(2,1)S(1)}, u32[]{:S(2)}, u32[]{:S(2)}) collective-permute-start(bf16[408,384]{1,0:T(8,128)(2,1)S(1)} %get-tuple-element.78), channel_id=1, source_target_pairs={{0,20},{4,16},{8,28},{12,24},{16,4},{20,0},{24,12},{28,8},{32,52},... | collective-permute-start | bytes 940040 | tf_op jit(solution)/shard_map/ppermute | solution.py:338
  13.7 3.1 %collective-permute-start.25 = (bf16[408,384]{1,0:T(8,128)(2,1)S(1)}, bf16[408,384]{1,0:T(8,128)(2,1)S(1)}, u32[]{:S(2)}, u32[]{:S(2)}) collective-permute-start(bf16[408,384]{1,0:T(8,128)(2,1)S(1)} %get-tuple-element.79), channel_id=1, source_target_pairs={{0,24},{4,28},{8,0},{12,4},{16,8},{20,12},{24,16},{28,20},{32,56},... | collective-permute-start | bytes 940040 | tf_op jit(solution)/shard_map/ppermute | solution.py:338
  16.8 11.2 %collective-permute-done.21.refs_2_ = bf16[408,384]{1,0:T(8,128)(2,1)S(1)} collective-permute-done((bf16[408,384]{1,0:T(8,128)(2,1)S(1)}, bf16[408,384]{1,0:T(8,128)(2,1)S(1)}, u32[]{:S(2)}, u32[]{:S(2)}) %collective-permute-start.21) | collective-permute-done | bytes 313376 | tf_op jit(solution)/shard_map/ppermute | solution.py:338
  28.0 3.6 %collective-permute-start.26 = (bf16[408,384]{1,0:T(8,128)(2,1)S(1)}, bf16[408,384]{1,0:T(8,128)(2,1)S(1)}, u32[]{:S(2)}, u32[]{:S(2)}) collective-permute-start(bf16[408,384]{1,0:T(8,128)(2,1)S(1)} %get-tuple-element.80), channel_id=1, source_target_pairs={{0,28},{4,24},{8,4},{12,0},{16,12},{20,8},{24,20},{28,16},{32,60},... | collective-permute-start | bytes 940040 | tf_op jit(solution)/shard_map/ppermute | solution.py:338
  31.7 4.8 %collective-permute-done.23.refs_4_ = bf16[408,384]{1,0:T(8,128)(2,1)S(1)} collective-permute-done((bf16[408,384]{1,0:T(8,128)(2,1)S(1)}, bf16[408,384]{1,0:T(8,128)(2,1)S(1)}, u32[]{:S(2)}, u32[]{:S(2)}) %collective-permute-start.23) | collective-permute-done | bytes 313376 | tf_op jit(solution)/shard_map/ppermute | solution.py:338
  37.3 2.0 %collective-permute-start.27 = (bf16[960,384]{1,0:T(8,128)(2,1)S(1)}, bf16[960,384]{1,0:T(8,128)(2,1)S(1)}, u32[]{:S(2)}, u32[]{:S(2)}) collective-permute-start(bf16[960,384]{1,0:T(8,128)(2,1)S(1)} %get-tuple-element.82), channel_id=1, source_target_pairs={{0,32},{4,36},{8,40},{12,44},{16,48},{20,52},{24,56},{28,60},{32,6... | collective-permute-start | bytes 2211848 | tf_op jit(solution)/shard_map/ppermute | solution.py:338
  39.3 3.8 %pack_ac.1 = (bf16[1040,384]{1,0:T(8,128)(2,1)S(1)}, bf16[1040,384]{1,0:T(8,128)(2,1)S(1)}, bf16[1040,384]{1,0:T(8,128)(2,1)S(1)}, bf16[1040,384]{1,0:T(8,128)(2...) custom-call(bf16[384,3072]{1,0:T(8,128)(2,1)} %wq.1, ...), custom_call_target="tpu_custom_call" | custom-call | tf_op jit(solution)/shard_map/pack_ac/pallas_call | solution.py:102
  44.7 5.0 %collective-permute-start.11 = (bf16[256,384]{1,0:T(8,128)(2,1)S(1)}, bf16[256,384]{1,0:T(8,128)(2,1)S(1)}, u32[]{:S(2)}, u32[]{:S(2)}) collective-permute-start(bf16[256,384]{1,0:T(8,128)(2,1)S(1)} %get-tuple-element.63), channel_id=1, source_target_pairs={{0,8},{4,12},{8,16},{12,20},{16,24},{20,28},{24,0},{28,4},{32,40},... | collective-permute-start | bytes 589832 | tf_op jit(solution)/shard_map/ppermute | solution.py:338
  49.6 3.3 %collective-permute-start.12 = (bf16[256,384]{1,0:T(8,128)(2,1)S(1)}, bf16[256,384]{1,0:T(8,128)(2,1)S(1)}, u32[]{:S(2)}, u32[]{:S(2)}) collective-permute-start(bf16[256,384]{1,0:T(8,128)(2,1)S(1)} %get-tuple-element.64), channel_id=1, source_target_pairs={{0,12},{4,8},{8,20},{12,16},{16,28},{20,24},{24,4},{28,0},{32,44},... | collective-permute-start | bytes 589832 | tf_op jit(solution)/shard_map/ppermute | solution.py:338
  52.9 5.2 %collective-permute-start.28 = (bf16[960,384]{1,0:T(8,128)(2,1)S(1)}, bf16[960,384]{1,0:T(8,128)(2,1)S(1)}, u32[]{:S(2)}, u32[]{:S(2)}) collective-permute-start(bf16[960,384]{1,0:T(8,128)(2,1)S(1)} %get-tuple-element.83), channel_id=1, source_target_pairs={{0,64},{4,68},{8,72},{12,76},{16,80},{20,84},{24,88},{28,92},{32,9... | collective-permute-start | bytes 2211848 | tf_op jit(solution)/shard_map/ppermute | solution.py:338
  58.1 5.2 %collective-permute-start.14 = (bf16[256,384]{1,0:T(8,128)(2,1)S(1)}, bf16[256,384]{1,0:T(8,128)(2,1)S(1)}, u32[]{:S(2)}, u32[]{:S(2)}) collective-permute-start(bf16[256,384]{1,0:T(8,128)(2,1)S(1)} %get-tuple-element.66), channel_id=1, source_target_pairs={{0,20},{4,16},{8,28},{12,24},{16,4},{20,0},{24,12},{28,8},{32,52},... | collective-permute-start | bytes 589832 | tf_op jit(solution)/shard_map/ppermute | solution.py:338
  64.8 2.1 %collective-permute-done.14.refs_5_ = bf16[256,384]{1,0:T(8,128)(2,1)S(1)} collective-permute-done((bf16[256,384]{1,0:T(8,128)(2,1)S(1)}, bf16[256,384]{1,0:T(8,128)(2,1)S(1)}, u32[]{:S(2)}, u32[]{:S(2)}) %collective-permute-start.14) | collective-permute-done | bytes 196640 | tf_op jit(solution)/shard_map/ppermute | solution.py:338
  67.0 3.3 %collective-permute-start.29 = (bf16[960,384]{1,0:T(8,128)(2,1)S(1)}, bf16[960,384]{1,0:T(8,128)(2,1)S(1)}, u32[]{:S(2)}, u32[]{:S(2)}) collective-permute-start(bf16[960,384]{1,0:T(8,128)(2,1)S(1)} %get-tuple-element.84), channel_id=1, source_target_pairs={{0,96},{4,100},{8,104},{12,108},{16,112},{20,116},{24,120},{28,124... | collective-permute-start | bytes 2211848 | tf_op jit(solution)/shard_map/ppermute | solution.py:338
  71.1 3.6 %collective-permute-start = (bf16[1040,384]{1,0:T(8,128)(2,1)S(1)}, bf16[1040,384]{1,0:T(8,128)(2,1)S(1)}, u32[]{:S(2)}, u32[]{:S(2)}) collective-permute-start(bf16[1040,384]{1,0:T(8,128)(2,1)S(1)} %get-tuple-element.50), channel_id=1, source_target_pairs={{0,32},{4,36},{8,40},{12,44},{16,48},{20,52},{24,56},{28,60},{32,6... | collective-permute-start | bytes 2396168 | tf_op jit(solution)/shard_map/ppermute | solution.py:338
  74.7 1.7 collective-permute-start.1
  76.4 2.6 %collective-permute-start.2 = (bf16[1040,384]{1,0:T(8,128)(2,1)S(1)}, bf16[1040,384]{1,0:T(8,128)(2,1)S(1)}, u32[]{:S(2)}, u32[]{:S(2)}) collective-permute-start(bf16[1040,384]{1,0:T(8,128)(2,1)S(1)} %get-tuple-element.52), channel_id=1, source_target_pairs={{0,96},{4,100},{8,104},{12,108},{16,112},{20,116},{24,120},{28,124... | collective-permute-start | bytes 2396168 | tf_op jit(solution)/shard_map/ppermute | solution.py:338
  79.3 24.6 %collective-permute-done.29.refs_3_ = bf16[960,384]{1,0:T(8,128)(2,1)S(1)} collective-permute-done((bf16[960,384]{1,0:T(8,128)(2,1)S(1)}, bf16[960,384]{1,0:T(8,128)(2,1)S(1)}, u32[]{:S(2)}, u32[]{:S(2)}) %collective-permute-start.29) | collective-permute-done | bytes 737312 | tf_op jit(solution)/shard_map/ppermute | solution.py:338
  104.0 4.2 %collective-permute-done.refs_1_ = bf16[1040,384]{1,0:T(8,128)(2,1)S(1)} collective-permute-done((bf16[1040,384]{1,0:T(8,128)(2,1)S(1)}, bf16[1040,384]{1,0:T(8,128)(2,1)S(1)}, u32[]{:S(2)}, u32[]{:S(2)}) %collective-permute-start) | collective-permute-done | bytes 798752 | tf_op jit(solution)/shard_map/ppermute | solution.py:338
  108.2 3.5 %collective-permute-done.1.refs_2_ = bf16[1040,384]{1,0:T(8,128)(2,1)S(1)} collective-permute-done((bf16[1040,384]{1,0:T(8,128)(2,1)S(1)}, bf16[1040,384]{1,0:T(8,128)(2,1)S(1)}, u32[]{:S(2)}, u32[]{:S(2)}) %collective-permute-start.1) | collective-permute-done | bytes 798752 | tf_op jit(solution)/shard_map/ppermute | solution.py:338
  111.7 5.4 %collective-permute-done.2.refs_3_ = bf16[1040,384]{1,0:T(8,128)(2,1)S(1)} collective-permute-done((bf16[1040,384]{1,0:T(8,128)(2,1)S(1)}, bf16[1040,384]{1,0:T(8,128)(2,1)S(1)}, u32[]{:S(2)}, u32[]{:S(2)}) %collective-permute-start.2) | collective-permute-done | bytes 798752 | tf_op jit(solution)/shard_map/ppermute | solution.py:338
  118.1 1.7 collective-permute-start.4
  119.8 2.1 %collective-permute-start.18 = (bf16[512,384]{1,0:T(8,128)(2,1)S(1)}, bf16[512,384]{1,0:T(8,128)(2,1)S(1)}, u32[]{:S(2)}, u32[]{:S(2)}) collective-permute-start(bf16[512,384]{1,0:T(8,128)(2,1)S(1)} %get-tuple-element.71), channel_id=1, source_target_pairs={{0,64},{4,68},{8,72},{12,76},{16,80},{20,84},{24,88},{28,92},{32,9... | collective-permute-start | bytes 1179656 | tf_op jit(solution)/shard_map/ppermute | solution.py:338
  121.9 5.5 %collective-permute-start.19 = (bf16[512,384]{1,0:T(8,128)(2,1)S(1)}, bf16[512,384]{1,0:T(8,128)(2,1)S(1)}, u32[]{:S(2)}, u32[]{:S(2)}) collective-permute-start(bf16[512,384]{1,0:T(8,128)(2,1)S(1)} %get-tuple-element.72), channel_id=1, source_target_pairs={{0,96},{4,100},{8,104},{12,108},{16,112},{20,116},{24,120},{28,124... | collective-permute-start | bytes 1179656 | tf_op jit(solution)/shard_map/ppermute | solution.py:338
  129.1 5.8 %collective-permute-start.5 = (bf16[576,384]{1,0:T(8,128)(2,1)S(1)}, bf16[576,384]{1,0:T(8,128)(2,1)S(1)}, u32[]{:S(2)}, u32[]{:S(2)}) collective-permute-start(bf16[576,384]{1,0:T(8,128)(2,1)S(1)} %get-tuple-element.56), channel_id=1, source_target_pairs={{0,12},{4,8},{8,20},{12,16},{16,28},{20,24},{24,4},{28,0},{32,44},... | collective-permute-start | bytes 1327112 | tf_op jit(solution)/shard_map/ppermute | solution.py:338
  134.9 3.4 %collective-permute-done.19.refs_11_ = bf16[512,384]{1,0:T(8,128)(2,1)S(1)} collective-permute-done((bf16[512,384]{1,0:T(8,128)(2,1)S(1)}, bf16[512,384]{1,0:T(8,128)(2,1)S(1)}, u32[]{:S(2)}, u32[]{:S(2)}) %collective-permute-start.19) | collective-permute-done | bytes 393248 | tf_op jit(solution)/shard_map/ppermute | solution.py:338
  138.6 2.9 %collective-permute-start.7 = (bf16[576,384]{1,0:T(8,128)(2,1)S(1)}, bf16[576,384]{1,0:T(8,128)(2,1)S(1)}, u32[]{:S(2)}, u32[]{:S(2)}) collective-permute-start(bf16[576,384]{1,0:T(8,128)(2,1)S(1)} %get-tuple-element.58), channel_id=1, source_target_pairs={{0,20},{4,16},{8,28},{12,24},{16,4},{20,0},{24,12},{28,8},{32,52},... | collective-permute-start | bytes 1327112 | tf_op jit(solution)/shard_map/ppermute | solution.py:338
  142.3 18.4 %collective-permute-start.9 = (bf16[576,384]{1,0:T(8,128)(2,1)S(1)}, bf16[576,384]{1,0:T(8,128)(2,1)S(1)}, u32[]{:S(2)}, u32[]{:S(2)}) collective-permute-start(bf16[576,384]{1,0:T(8,128)(2,1)S(1)} %get-tuple-element.60), channel_id=1, source_target_pairs={{0,28},{4,24},{8,4},{12,0},{16,12},{20,8},{24,20},{28,16},{32,60},... | collective-permute-start | bytes 1327112 | tf_op jit(solution)/shard_map/ppermute | solution.py:338
  160.7 2.9 %shard_map.150 = (bf16[96,12288]{1,0:T(8,128)(2,1)}, f32[1,96]{1,0:T(1,128)}) custom-call(bf16[960,384]{1,0:T(8,128)(2,1)S(1)} %get-tuple-element.81.refs_0_, bf16[960,384]{1,0:T(8,128)(2,1)S(1)} %collective-permute-done.27.refs_1_, bf16[960,384]{1,0:T(8,128)(2,1)S(1)} %collective-permute-done.28.refs_2_, ...), custom_call_target="tpu_custom_call" | custom-call | tf_op jit(solution)/shard_map/pallas_call | solution.py:301
  163.6 10.4 %collective-permute-done.8.refs_6_ = bf16[576,384]{1,0:T(8,128)(2,1)S(1)} collective-permute-done((bf16[576,384]{1,0:T(8,128)(2,1)S(1)}, bf16[576,384]{1,0:T(8,128)(2,1)S(1)}, u32[]{:S(2)}, u32[]{:S(2)}) %collective-permute-start.8) | collective-permute-done | bytes 442400 | tf_op jit(solution)/shard_map/ppermute | solution.py:338
  174.0 4.3 %shard_map.149 = (bf16[96,12288]{1,0:T(8,128)(2,1)}, bf16[96,12288]{1,0:T(8,128)(2,1)}, f32[1,96]{1,0:T(1,128)}, f32[1,96]{1,0:T(1,128)}) custom-call(bf16[576,384]{1,0:T(8,128)(2,1)S(1)} %get-tuple-element.53.refs_0_, bf16[576,384]{1,0:T(8,128)(2,1)S(1)} %collective-permute-done.3.refs_1_, bf16[576,384]{1,0:T(8,128)(2,1)S(1)} %collective-permute-done.4.refs_2_, ...), custom_call_target="tpu_custom_call" | custom-call | tf_op jit(solution)/shard_map/pallas_call | solution.py:301
  (38 shorter events, 14.5 us)
Async XLA Ops:
  3.3 10.4 %collective-permute-start.20 = (bf16[408,384]{1,0:T(8,128)(2,1)S(1)}, bf16[408,384]{1,0:T(8,128)(2,1)S(1)}, u32[]{:S(2)}, u32[]{:S(2)}) collective-permute-start(bf16[408,384]{1,0:T(8,128)(2,1)S(1)} %get-tuple-element.74), channel_id=1, source_target_pairs={{0,4},{4,0},{8,12},{12,8},{16,20},{20,16},{24,28},{28,24},{32,36},... | collective-permute-start | bytes 940040 | tf_op jit(solution)/shard_map/ppermute | solution.py:338
  5.0 23.0 %collective-permute-start.21 = (bf16[408,384]{1,0:T(8,128)(2,1)S(1)}, bf16[408,384]{1,0:T(8,128)(2,1)S(1)}, u32[]{:S(2)}, u32[]{:S(2)}) collective-permute-start(bf16[408,384]{1,0:T(8,128)(2,1)S(1)} %get-tuple-element.75), channel_id=1, source_target_pairs={{0,8},{4,12},{8,16},{12,20},{16,24},{20,28},{24,0},{28,4},{32,40},... | collective-permute-start | bytes 940040 | tf_op jit(solution)/shard_map/ppermute | solution.py:338
  6.6 25.1 %collective-permute-start.22 = (bf16[408,384]{1,0:T(8,128)(2,1)S(1)}, bf16[408,384]{1,0:T(8,128)(2,1)S(1)}, u32[]{:S(2)}, u32[]{:S(2)}) collective-permute-start(bf16[408,384]{1,0:T(8,128)(2,1)S(1)} %get-tuple-element.76), channel_id=1, source_target_pairs={{0,12},{4,8},{8,20},{12,16},{16,28},{20,24},{24,4},{28,0},{32,44},... | collective-permute-start | bytes 940040 | tf_op jit(solution)/shard_map/ppermute | solution.py:338
  8.1 28.3 %collective-permute-start.23 = (bf16[408,384]{1,0:T(8,128)(2,1)S(1)}, bf16[408,384]{1,0:T(8,128)(2,1)S(1)}, u32[]{:S(2)}, u32[]{:S(2)}) collective-permute-start(bf16[408,384]{1,0:T(8,128)(2,1)S(1)} %get-tuple-element.77), channel_id=1, source_target_pairs={{0,16},{4,20},{8,24},{12,28},{16,0},{20,4},{24,8},{28,12},{32,48},... | collective-permute-start | bytes 940040 | tf_op jit(solution)/shard_map/ppermute | solution.py:338
  9.6 26.9 %collective-permute-start.24 = (bf16[408,384]{1,0:T(8,128)(2,1)S(1)}, bf16[408,384]{1,0:T(8,128)(2,1)S(1)}, u32[]{:S(2)}, u32[]{:S(2)}) collective-permute-start(bf16[408,384]{1,0:T(8,128)(2,1)S(1)} %get-tuple-element.78), channel_id=1, source_target_pairs={{0,20},{4,16},{8,28},{12,24},{16,4},{20,0},{24,12},{28,8},{32,52},... | collective-permute-start | bytes 940040 | tf_op jit(solution)/shard_map/ppermute | solution.py:338
  13.7 23.4 %collective-permute-start.25 = (bf16[408,384]{1,0:T(8,128)(2,1)S(1)}, bf16[408,384]{1,0:T(8,128)(2,1)S(1)}, u32[]{:S(2)}, u32[]{:S(2)}) collective-permute-start(bf16[408,384]{1,0:T(8,128)(2,1)S(1)} %get-tuple-element.79), channel_id=1, source_target_pairs={{0,24},{4,28},{8,0},{12,4},{16,8},{20,12},{24,16},{28,20},{32,56},... | collective-permute-start | bytes 940040 | tf_op jit(solution)/shard_map/ppermute | solution.py:338
  28.0 9.0 %collective-permute-start.26 = (bf16[408,384]{1,0:T(8,128)(2,1)S(1)}, bf16[408,384]{1,0:T(8,128)(2,1)S(1)}, u32[]{:S(2)}, u32[]{:S(2)}) collective-permute-start(bf16[408,384]{1,0:T(8,128)(2,1)S(1)} %get-tuple-element.80), channel_id=1, source_target_pairs={{0,28},{4,24},{8,4},{12,0},{16,12},{20,8},{24,20},{28,16},{32,60},... | collective-permute-start | bytes 940040 | tf_op jit(solution)/shard_map/ppermute | solution.py:338
  37.3 39.1 %collective-permute-start.27 = (bf16[960,384]{1,0:T(8,128)(2,1)S(1)}, bf16[960,384]{1,0:T(8,128)(2,1)S(1)}, u32[]{:S(2)}, u32[]{:S(2)}) collective-permute-start(bf16[960,384]{1,0:T(8,128)(2,1)S(1)} %get-tuple-element.82), channel_id=1, source_target_pairs={{0,32},{4,36},{8,40},{12,44},{16,48},{20,52},{24,56},{28,60},{32,6... | collective-permute-start | bytes 2211848 | tf_op jit(solution)/shard_map/ppermute | solution.py:338
  43.1 9.8 %collective-permute-start.10 = (bf16[256,384]{1,0:T(8,128)(2,1)S(1)}, bf16[256,384]{1,0:T(8,128)(2,1)S(1)}, u32[]{:S(2)}, u32[]{:S(2)}) collective-permute-start(bf16[256,384]{1,0:T(8,128)(2,1)S(1)} %get-tuple-element.62), channel_id=1, source_target_pairs={{0,4},{4,0},{8,12},{12,8},{16,20},{20,16},{24,28},{28,24},{32,36},... | collective-permute-start | bytes 589832 | tf_op jit(solution)/shard_map/ppermute | solution.py:338
  44.7 13.4 %collective-permute-start.11 = (bf16[256,384]{1,0:T(8,128)(2,1)S(1)}, bf16[256,384]{1,0:T(8,128)(2,1)S(1)}, u32[]{:S(2)}, u32[]{:S(2)}) collective-permute-start(bf16[256,384]{1,0:T(8,128)(2,1)S(1)} %get-tuple-element.63), channel_id=1, source_target_pairs={{0,8},{4,12},{8,16},{12,20},{16,24},{20,28},{24,0},{28,4},{32,40},... | collective-permute-start | bytes 589832 | tf_op jit(solution)/shard_map/ppermute | solution.py:338
  49.6 13.7 %collective-permute-start.12 = (bf16[256,384]{1,0:T(8,128)(2,1)S(1)}, bf16[256,384]{1,0:T(8,128)(2,1)S(1)}, u32[]{:S(2)}, u32[]{:S(2)}) collective-permute-start(bf16[256,384]{1,0:T(8,128)(2,1)S(1)} %get-tuple-element.64), channel_id=1, source_target_pairs={{0,12},{4,8},{8,20},{12,16},{16,28},{20,24},{24,4},{28,0},{32,44},... | collective-permute-start | bytes 589832 | tf_op jit(solution)/shard_map/ppermute | solution.py:338
  52.9 10.4 %collective-permute-start.13 = (bf16[256,384]{1,0:T(8,128)(2,1)S(1)}, bf16[256,384]{1,0:T(8,128)(2,1)S(1)}, u32[]{:S(2)}, u32[]{:S(2)}) collective-permute-start(bf16[256,384]{1,0:T(8,128)(2,1)S(1)} %get-tuple-element.65), channel_id=1, source_target_pairs={{0,16},{4,20},{8,24},{12,28},{16,0},{20,4},{24,8},{28,12},{32,48},... | collective-permute-start | bytes 589832 | tf_op jit(solution)/shard_map/ppermute | solution.py:338
  52.9 26.3 %collective-permute-start.28 = (bf16[960,384]{1,0:T(8,128)(2,1)S(1)}, bf16[960,384]{1,0:T(8,128)(2,1)S(1)}, u32[]{:S(2)}, u32[]{:S(2)}) collective-permute-start(bf16[960,384]{1,0:T(8,128)(2,1)S(1)} %get-tuple-element.83), channel_id=1, source_target_pairs={{0,64},{4,68},{8,72},{12,76},{16,80},{20,84},{24,88},{28,92},{32,9... | collective-permute-start | bytes 2211848 | tf_op jit(solution)/shard_map/ppermute | solution.py:338
  58.1 8.9 %collective-permute-start.14 = (bf16[256,384]{1,0:T(8,128)(2,1)S(1)}, bf16[256,384]{1,0:T(8,128)(2,1)S(1)}, u32[]{:S(2)}, u32[]{:S(2)}) collective-permute-start(bf16[256,384]{1,0:T(8,128)(2,1)S(1)} %get-tuple-element.66), channel_id=1, source_target_pairs={{0,20},{4,16},{8,28},{12,24},{16,4},{20,0},{24,12},{28,8},{32,52},... | collective-permute-start | bytes 589832 | tf_op jit(solution)/shard_map/ppermute | solution.py:338
  63.3 7.8 %collective-permute-start.15 = (bf16[256,384]{1,0:T(8,128)(2,1)S(1)}, bf16[256,384]{1,0:T(8,128)(2,1)S(1)}, u32[]{:S(2)}, u32[]{:S(2)}) collective-permute-start(bf16[256,384]{1,0:T(8,128)(2,1)S(1)} %get-tuple-element.67), channel_id=1, source_target_pairs={{0,24},{4,28},{8,0},{12,4},{16,8},{20,12},{24,16},{28,20},{32,56},... | collective-permute-start | bytes 589832 | tf_op jit(solution)/shard_map/ppermute | solution.py:338
  63.3 11.4 %collective-permute-start.16 = (bf16[256,384]{1,0:T(8,128)(2,1)S(1)}, bf16[256,384]{1,0:T(8,128)(2,1)S(1)}, u32[]{:S(2)}, u32[]{:S(2)}) collective-permute-start(bf16[256,384]{1,0:T(8,128)(2,1)S(1)} %get-tuple-element.68), channel_id=1, source_target_pairs={{0,28},{4,24},{8,4},{12,0},{16,12},{20,8},{24,20},{28,16},{32,60},... | collective-permute-start | bytes 589832 | tf_op jit(solution)/shard_map/ppermute | solution.py:338
  67.0 36.9 %collective-permute-start.29 = (bf16[960,384]{1,0:T(8,128)(2,1)S(1)}, bf16[960,384]{1,0:T(8,128)(2,1)S(1)}, u32[]{:S(2)}, u32[]{:S(2)}) collective-permute-start(bf16[960,384]{1,0:T(8,128)(2,1)S(1)} %get-tuple-element.84), channel_id=1, source_target_pairs={{0,96},{4,100},{8,104},{12,108},{16,112},{20,116},{24,120},{28,124... | collective-permute-start | bytes 2211848 | tf_op jit(solution)/shard_map/ppermute | solution.py:338
  71.1 37.1 %collective-permute-start = (bf16[1040,384]{1,0:T(8,128)(2,1)S(1)}, bf16[1040,384]{1,0:T(8,128)(2,1)S(1)}, u32[]{:S(2)}, u32[]{:S(2)}) collective-permute-start(bf16[1040,384]{1,0:T(8,128)(2,1)S(1)} %get-tuple-element.50), channel_id=1, source_target_pairs={{0,32},{4,36},{8,40},{12,44},{16,48},{20,52},{24,56},{28,60},{32,6... | collective-permute-start | bytes 2396168 | tf_op jit(solution)/shard_map/ppermute | solution.py:338
  74.7 37.0 %collective-permute-start.1 = (bf16[1040,384]{1,0:T(8,128)(2,1)S(1)}, bf16[1040,384]{1,0:T(8,128)(2,1)S(1)}, u32[]{:S(2)}, u32[]{:S(2)}) collective-permute-start(bf16[1040,384]{1,0:T(8,128)(2,1)S(1)} %get-tuple-element.51), channel_id=1, source_target_pairs={{0,64},{4,68},{8,72},{12,76},{16,80},{20,84},{24,88},{28,92},{32,9... | collective-permute-start | bytes 2396168 | tf_op jit(solution)/shard_map/ppermute | solution.py:338
  76.4 40.7 %collective-permute-start.2 = (bf16[1040,384]{1,0:T(8,128)(2,1)S(1)}, bf16[1040,384]{1,0:T(8,128)(2,1)S(1)}, u32[]{:S(2)}, u32[]{:S(2)}) collective-permute-start(bf16[1040,384]{1,0:T(8,128)(2,1)S(1)} %get-tuple-element.52), channel_id=1, source_target_pairs={{0,96},{4,100},{8,104},{12,108},{16,112},{20,116},{24,120},{28,124... | collective-permute-start | bytes 2396168 | tf_op jit(solution)/shard_map/ppermute | solution.py:338
  79.2 42.7 %collective-permute-start.17 = (bf16[512,384]{1,0:T(8,128)(2,1)S(1)}, bf16[512,384]{1,0:T(8,128)(2,1)S(1)}, u32[]{:S(2)}, u32[]{:S(2)}) collective-permute-start(bf16[512,384]{1,0:T(8,128)(2,1)S(1)} %get-tuple-element.70), channel_id=1, source_target_pairs={{0,32},{4,36},{8,40},{12,44},{16,48},{20,52},{24,56},{28,60},{32,6... | collective-permute-start | bytes 1179656 | tf_op jit(solution)/shard_map/ppermute | solution.py:338
  103.9 38.4 %collective-permute-start.30 = (bf16[768,384]{1,0:T(8,128)(2,1)S(1)}, bf16[768,384]{1,0:T(8,128)(2,1)S(1)}, u32[]{:S(2)}, u32[]{:S(2)}) collective-permute-start(bf16[768,384]{1,0:T(8,128)(2,1)S(1)} %shard_map.148.refs_12_), channel_id=1, source_target_pairs={{0,1},{1,0},{2,3},{3,2},{4,5},{5,4},{6,7},{7,6},{8,9},{9,8},{10,11... | collective-permute-start | bytes 1769480 | tf_op jit(solution)/shard_map/ppermute | solution.py:375
  117.4 21.2 %collective-permute-start.3 = (bf16[576,384]{1,0:T(8,128)(2,1)S(1)}, bf16[576,384]{1,0:T(8,128)(2,1)S(1)}, u32[]{:S(2)}, u32[]{:S(2)}) collective-permute-start(bf16[576,384]{1,0:T(8,128)(2,1)S(1)} %get-tuple-element.54), channel_id=1, source_target_pairs={{0,4},{4,0},{8,12},{12,8},{16,20},{20,16},{24,28},{28,24},{32,36},... | collective-permute-start | bytes 1327112 | tf_op jit(solution)/shard_map/ppermute | solution.py:338
  118.1 23.5 %collective-permute-start.4 = (bf16[576,384]{1,0:T(8,128)(2,1)S(1)}, bf16[576,384]{1,0:T(8,128)(2,1)S(1)}, u32[]{:S(2)}, u32[]{:S(2)}) collective-permute-start(bf16[576,384]{1,0:T(8,128)(2,1)S(1)} %get-tuple-element.55), channel_id=1, source_target_pairs={{0,8},{4,12},{8,16},{12,20},{16,24},{20,28},{24,0},{28,4},{32,40},... | collective-permute-start | bytes 1327112 | tf_op jit(solution)/shard_map/ppermute | solution.py:338
  119.8 9.3 %collective-permute-start.18 = (bf16[512,384]{1,0:T(8,128)(2,1)S(1)}, bf16[512,384]{1,0:T(8,128)(2,1)S(1)}, u32[]{:S(2)}, u32[]{:S(2)}) collective-permute-start(bf16[512,384]{1,0:T(8,128)(2,1)S(1)} %get-tuple-element.71), channel_id=1, source_target_pairs={{0,64},{4,68},{8,72},{12,76},{16,80},{20,84},{24,88},{28,92},{32,9... | collective-permute-start | bytes 1179656 | tf_op jit(solution)/shard_map/ppermute | solution.py:338
  121.9 16.4 %collective-permute-start.19 = (bf16[512,384]{1,0:T(8,128)(2,1)S(1)}, bf16[512,384]{1,0:T(8,128)(2,1)S(1)}, u32[]{:S(2)}, u32[]{:S(2)}) collective-permute-start(bf16[512,384]{1,0:T(8,128)(2,1)S(1)} %get-tuple-element.72), channel_id=1, source_target_pairs={{0,96},{4,100},{8,104},{12,108},{16,112},{20,116},{24,120},{28,124... | collective-permute-start | bytes 1179656 | tf_op jit(solution)/shard_map/ppermute | solution.py:338
  129.1 34.5 %collective-permute-start.5 = (bf16[576,384]{1,0:T(8,128)(2,1)S(1)}, bf16[576,384]{1,0:T(8,128)(2,1)S(1)}, u32[]{:S(2)}, u32[]{:S(2)}) collective-permute-start(bf16[576,384]{1,0:T(8,128)(2,1)S(1)} %get-tuple-element.56), channel_id=1, source_target_pairs={{0,12},{4,8},{8,20},{12,16},{16,28},{20,24},{24,4},{28,0},{32,44},... | collective-permute-start | bytes 1327112 | tf_op jit(solution)/shard_map/ppermute | solution.py:338
  138.3 25.3 %collective-permute-start.6 = (bf16[576,384]{1,0:T(8,128)(2,1)S(1)}, bf16[576,384]{1,0:T(8,128)(2,1)S(1)}, u32[]{:S(2)}, u32[]{:S(2)}) collective-permute-start(bf16[576,384]{1,0:T(8,128)(2,1)S(1)} %get-tuple-element.57), channel_id=1, source_target_pairs={{0,16},{4,20},{8,24},{12,28},{16,0},{20,4},{24,8},{28,12},{32,48},... | collective-permute-start | bytes 1327112 | tf_op jit(solution)/shard_map/ppermute | solution.py:338
  138.6 25.0 %collective-permute-start.7 = (bf16[576,384]{1,0:T(8,128)(2,1)S(1)}, bf16[576,384]{1,0:T(8,128)(2,1)S(1)}, u32[]{:S(2)}, u32[]{:S(2)}) collective-permute-start(bf16[576,384]{1,0:T(8,128)(2,1)S(1)} %get-tuple-element.58), channel_id=1, source_target_pairs={{0,20},{4,16},{8,28},{12,24},{16,4},{20,0},{24,12},{28,8},{32,52},... | collective-permute-start | bytes 1327112 | tf_op jit(solution)/shard_map/ppermute | solution.py:338
  141.5 32.5 %collective-permute-start.8 = (bf16[576,384]{1,0:T(8,128)(2,1)S(1)}, bf16[576,384]{1,0:T(8,128)(2,1)S(1)}, u32[]{:S(2)}, u32[]{:S(2)}) collective-permute-start(bf16[576,384]{1,0:T(8,128)(2,1)S(1)} %get-tuple-element.59), channel_id=1, source_target_pairs={{0,24},{4,28},{8,0},{12,4},{16,8},{20,12},{24,16},{28,20},{32,56},... | collective-permute-start | bytes 1327112 | tf_op jit(solution)/shard_map/ppermute | solution.py:338
  142.3 31.7 %collective-permute-start.9 = (bf16[576,384]{1,0:T(8,128)(2,1)S(1)}, bf16[576,384]{1,0:T(8,128)(2,1)S(1)}, u32[]{:S(2)}, u32[]{:S(2)}) collective-permute-start(bf16[576,384]{1,0:T(8,128)(2,1)S(1)} %get-tuple-element.60), channel_id=1, source_target_pairs={{0,28},{4,24},{8,4},{12,0},{16,12},{20,8},{24,20},{28,16},{32,60},... | collective-permute-start | bytes 1327112 | tf_op jit(solution)/shard_map/ppermute | solution.py:338

commit v4 on v0

v4 whole, which is shorter than its diff:
```python
import functools

import jax
import jax.numpy as jnp
from jax import lax
from jax.experimental import pallas as pl
from jax.experimental.pallas import tpu as pltpu
from jax.sharding import PartitionSpec as P


SIDE = 4
PLANE = 8
PEERS = SIDE * PLANE
GROUP = 4
LANES = 128
EARLY = 64
TAIL = 8
LATER_A = (0, 1, 3)
LATER_B = (0, 1, 2, 3, 6, 7)
HBM = pl.BlockSpec(memory_space=pltpu.HBM)
VMEM = pl.BlockSpec(memory_space=pltpu.VMEM)
PARAMS = pltpu.CompilerParams(vmem_limit_bytes=30 * 2**20)


def moved(place, dz, i):
    dy, dx = i // 2, i % 2
    z, y, x = place // PLANE, (place // 2) % SIDE, place % 2
    return ((z + dz) % SIDE) * PLANE + ((y + dy) % SIDE) * 2 + (x + dx) % 2


def came_from(place, dz, i):
    return moved(place, -dz % SIDE, (-(i // 2) % SIDE) * 2 + i % 2)


def far(x):
    return pltpu.with_memory_space_constraint(x, pltpu.HBM)


def shape(*dims):
    return jax.ShapeDtypeStruct(dims, jnp.bfloat16)


def split3(g):
    first = g.astype(jnp.bfloat16)
    rest = g - first.astype(jnp.float32)
    second = rest.astype(jnp.bfloat16)
    third = (rest - second.astype(jnp.float32)).astype(jnp.bfloat16)
    none = jnp.zeros((TAIL - 3, g.shape[1]), jnp.bfloat16)
    return jnp.concatenate([first, second, third, none], 0)


def low_of(core, low_k, low_v, lowbox, sem):
    even = pltpu.make_async_copy(low_k, lowbox, sem)
    odd = pltpu.make_async_copy(low_v, lowbox, sem)

    @pl.when(core == 0)
    def _():
        even.start()

    @pl.when(core == 1)
    def _():
        odd.start()

    return even


def turned(block, cols):
    t = block.T
    return [t[p * cols : (p + 1) * cols, :] for p in range(GROUP)]


def fill_b(lot, dz, weights, cols):
    lot[dz * cols : (dz + 1) * cols, :] = weights


def fill_b_tail(lot, low, parts, cols):
    rank = low.shape[0]
    lot[SIDE * cols : SIDE * cols + rank, :] = low
    lot[SIDE * cols + rank :, :] = parts


def pack_first_kernel(wq, wk, wv, low_q, low_k, low_v, gain, lot_a, b4, b5, *refs, cols):
    inbox, vbox, turn, vturn, qbox, lowbox, gbox, insem, vsem, lowsem = refs
    wide = GROUP * cols
    first = cols + EARLY
    place = lax.axis_index("shard")
    core = lax.axis_index("model") % 2
    z, y, x = place // PLANE, (place // 2) % SIDE, place % 2
    copies = []
    for h in range(2):
        at = pl.multiple_of((((z + 2) % SIDE) * 2 + h) * wide, LANES)
        for m, w in enumerate((wq, wk)):
            copies.append(
                pltpu.make_async_copy(w.at[:, pl.ds(at, wide)], inbox.at[m, h], insem.at[m, h])
            )
            copies[-1].start()
    vcopies = []
    for dz in range(SIDE):
        at = pl.multiple_of((((z + dz) % SIDE) * 2 + ((y + 2) % SIDE) // 2) * wide, LANES)
        vcopies.append(pltpu.make_async_copy(wv.at[:, pl.ds(at, wide)], vbox.at[dz], vsem.at[dz]))
        vcopies[-1].start()
    small = [
        pltpu.make_async_copy(low_q, qbox, lowsem.at[0]),
        pltpu.make_async_copy(gain, gbox, lowsem.at[1]),
    ]
    for copy in small:
        copy.start()
    small.append(low_of(core, low_k, low_v, lowbox, lowsem.at[2]))
    for copy in copies:
        copy.wait()
    for m in range(2):
        for h in range(2):
            for p, part in enumerate(turned(inbox[m, h], cols)):
                turn[h * GROUP + p, m * cols : (m + 1) * cols, :] = part
    for i in range(PLANE):
        to = moved(place, 0, i) % PLANE
        lot_a[i * first : (i + 1) * first, :] = turn[to, 0:first, :]
    for dz in range(SIDE):
        vcopies[dz].wait()
        for p, part in enumerate(turned(vbox[dz], cols)):
            vturn[dz * GROUP + p] = part
    for copy in small:
        copy.wait()
    lot_a[PLANE * first :, :] = qbox[...]
    parts = split3(gbox[...].reshape(1, -1))
    for dx, lot in enumerate((b4, b5)):
        for dz in range(SIDE):
            at = dz * GROUP + ((y + 2) % 2) * 2 + (x + dx) % 2
            fill_b(lot, dz, vturn[at], cols)
        fill_b_tail(lot, lowbox[...], parts, cols)


def pack_rest_kernel(wq, wk, wv, low_q, low_k, low_v, gain, *refs, cols):
    highs, refs = refs[:3], refs[3:]
    lot_a, refs = refs[: len(LATER_A)], refs[len(LATER_A) :]
    lot_b, refs = refs[: len(LATER_B)], refs[len(LATER_B) :]
    lot_c, mix, refs = refs[:PLANE], refs[PLANE], refs[PLANE + 1 :]
    inbox, turn, qbox, lowbox, gbox, highbox, insem, lowsem = refs
    wide = GROUP * cols
    first, rest = cols + EARLY, cols - EARLY
    width = wv.shape[1]
    place = lax.axis_index("shard")
    core = lax.axis_index("model") % 2
    start = place * cols
    base = jnp.minimum(start // LANES, width // LANES - 2) * LANES
    base = pl.multiple_of(base, LANES)
    copies = [
        [
            pltpu.make_async_copy(
                w.at[:, i * wide : (i + 1) * wide], inbox.at[m, i], insem.at[m, i]
            )
            for m, w in enumerate((wq, wk, wv))
        ]
        for i in range(PEERS // GROUP)
    ]
    for group in copies:
        for copy in group:
            copy.start()
    small = [
        pltpu.make_async_copy(high.at[:, pl.ds(base, 2 * LANES)], highbox.at[m], lowsem.at[m])
        for m, high in enumerate(highs)
    ]
    small.append(pltpu.make_async_copy(gain, gbox, lowsem.at[3]))
    small.append(pltpu.make_async_copy(low_q, qbox, lowsem.at[4]))
    for copy in small:
        copy.start()
    small.append(low_of(core, low_k, low_v, lowbox, lowsem.at[5]))
    for i in range(PEERS // GROUP):
        for m in range(3):
            copies[i][m].wait()
            for p, part in enumerate(turned(inbox[m, i], cols)):
                turn[i * GROUP + p, m * cols : (m + 1) * cols, :] = part
    for copy in small:
        copy.wait()
    at_col = lax.broadcasted_iota(jnp.int32, (cols, 2 * LANES), 0) + (start - base)
    pick = at_col == lax.broadcasted_iota(jnp.int32, (cols, 2 * LANES), 1)
    pick = pick.astype(jnp.bfloat16)
    same = (
        lax.broadcasted_iota(jnp.int32, (cols, cols), 0)
        == lax.broadcasted_iota(jnp.int32, (cols, cols), 1)
    ).astype(jnp.bfloat16)
    for m in range(3):
        own = lax.dot_general(
            pick, highbox[m], (((1,), (1,)), ((), ())), preferred_element_type=jnp.float32
        )
        mix[m] = jnp.concatenate([same, own.astype(jnp.bfloat16)], 1)
    parts = split3(gbox[...].reshape(1, -1))
    for lot, i in zip(lot_b, LATER_B):
        for dz in range(SIDE):
            fill_b(lot, dz, turn[moved(place, dz, i), 2 * cols : 3 * cols, :], cols)
        fill_b_tail(lot, lowbox[...], parts, cols)
    for lot, dz in zip(lot_a, LATER_A):
        lot[PLANE * first :, :] = qbox[...]
        for i in range(PLANE):
            lot[i * first : (i + 1) * first, :] = turn[moved(place, dz, i), 0:first, :]
    for i in range(PLANE):
        for dz in range(SIDE):
            lot_c[i][dz * rest : (dz + 1) * rest, :] = turn[
                moved(place, dz, i), first : 2 * cols, :
            ]


def pack(weights, lows, gain, highs):
    rows, width = weights[0].shape
    rank = lows[0].shape[0]
    cols = width // PEERS
    groups = PEERS // GROUP
    wide = GROUP * cols
    one_a = shape(PLANE * (cols + EARLY) + rank, rows)
    one_b = shape(SIDE * cols + rank + TAIL, rows)
    one_c = shape(SIDE * (cols - EARLY), rows)
    operands = [*map(far, weights), *map(far, lows), far(gain)]
    small = [
        pltpu.VMEM((rank, rows), jnp.bfloat16),
        pltpu.VMEM((rank, rows), jnp.bfloat16),
        pltpu.VMEM((rows,), jnp.float32),
    ]
    out = [one_a, one_b, one_b]
    lot_a, b4, b5 = pl.pallas_call(
        functools.partial(pack_first_kernel, cols=cols),
        in_specs=[HBM] * len(operands),
        out_specs=[VMEM] * len(out),
        out_shape=out,
        scratch_shapes=[
            pltpu.VMEM((2, 2, rows, wide), jnp.bfloat16),
            pltpu.VMEM((SIDE, rows, wide), jnp.bfloat16),
            pltpu.VMEM((PLANE, 2 * cols, rows), jnp.bfloat16),
            pltpu.VMEM((SIDE * GROUP, cols, rows), jnp.bfloat16),
            *small,
            pltpu.SemaphoreType.DMA((2, 2)),
            pltpu.SemaphoreType.DMA((SIDE,)),
            pltpu.SemaphoreType.DMA((3,)),
        ],
        compiler_params=PARAMS,
        name="pack_first",
    )(*operands)
    lots = {("a", 2): lot_a, ("b", 4): b4, ("b", 5): b5}
    operands += map(far, highs)
    names = [("a", k) for k in LATER_A] + [("b", k) for k in LATER_B]
    names += [("c", k) for k in range(PLANE)]
    out = [{"a": one_a, "b": one_b, "c": one_c}[name] for name, _ in names]
    out.append(shape(3, cols, cols + rank))
    *later, mix = pl.pallas_call(
        functools.partial(pack_rest_kernel, cols=cols),
        in_specs=[HBM] * len(operands),
        out_specs=[VMEM] * len(out),
        out_shape=out,
        scratch_shapes=[
            pltpu.VMEM((3, groups, rows, wide), jnp.bfloat16),
            pltpu.VMEM((PEERS, 3 * cols, rows), jnp.bfloat16),
            *small,
            pltpu.VMEM((3, rank, 2 * LANES), jnp.bfloat16),
            pltpu.SemaphoreType.DMA((3, groups)),
            pltpu.SemaphoreType.DMA((6,)),
        ],
        compiler_params=PARAMS,
        name="pack_rest",
    )(*operands)
    lots.update(zip(names, later))
    return (
        [lots["a", k] for k in range(SIDE)],
        [lots["b", k] for k in range(PLANE)],
        [lots["c", k] for k in range(PLANE)],
        mix,
    )


def repack_b(lot, cols, rank):
    rows = lot[0].shape[1]
    block = cols + rank
    tall = PLANE * block + 3 * PLANE

    def kernel(*refs):
        ins, outs = refs[:PLANE], refs[PLANE:]
        gains = [ref[SIDE * cols + rank :, :].astype(jnp.float32) for ref in ins]
        parts = [g[k : k + 1, :] for k in range(3) for g in gains]
        parts = jnp.concatenate(parts, 0).astype(jnp.bfloat16)
        for dz, out in enumerate(outs):
            for i, ref in enumerate(ins):
                at = i * block
                out[at : at + cols, :] = ref[dz * cols : (dz + 1) * cols, :]
                out[at + cols : at + block, :] = ref[SIDE * cols : SIDE * cols + rank, :]
            out[PLANE * block :, :] = parts

    return pl.pallas_call(
        kernel,
        in_specs=[VMEM] * PLANE,
        out_specs=[VMEM] * SIDE,
        out_shape=[shape(tall, rows)] * SIDE,
        compiler_params=PARAMS,
        name="repack_b",
    )(*lot)


def collect(lot, cols, rank):
    rows = lot[0].shape[1]
    block = cols + rank

    def kernel(*refs):
        ins, low, gain = refs[:SIDE], refs[SIDE], refs[SIDE + 1]
        for dz, ref in enumerate(ins):
            for i in range(PLANE):
                at = (dz * PLANE + i) * rank
                low[at : at + rank, :] = ref[i * block + cols : (i + 1) * block, :]
            g = ref[PLANE * block :, :].astype(jnp.float32)
            gain[dz * PLANE : (dz + 1) * PLANE, :] = (
                g[0:PLANE, :] + g[PLANE : 2 * PLANE, :] + g[2 * PLANE :, :]
            )

    return pl.pallas_call(
        kernel,
        in_specs=[VMEM] * SIDE,
        out_specs=[VMEM] * 2,
        out_shape=[shape(PEERS * rank, rows), jax.ShapeDtypeStruct((PEERS, rows), jnp.float32)],
        compiler_params=PARAMS,
        name="collect",
    )(*lot)


def repack(parts, moves, tall, count):
    def kernel(*refs):
        ins, outs = refs[: len(parts)], refs[len(parts) :]
        for k, to, j, at, n in moves:
            outs[k][to : to + n, :] = ins[j][at : at + n, :]

    out = [shape(tall, parts[0].shape[1])] * count
    return pl.pallas_call(
        kernel,
        in_specs=[VMEM] * len(parts),
        out_specs=[VMEM] * count,
        out_shape=out,
        compiler_params=PARAMS,
    )(*parts)


def place_all():
    return [(dz, i) for dz in range(SIDE) for i in range(PLANE)]


def merge(value_of, m, operands, gains, mix):
    _, cols, _ = mix.shape
    rows = gains.shape[1]
    count = len(operands)

    def kernel(*refs):
        ins, gain, both = refs[:count], refs[count], refs[count + 1]
        final, scale_ref, wide, outbox, outsem = refs[count + 2 :]
        place = lax.axis_index("shard")
        top = jnp.zeros((cols, rows), jnp.float32)
        for dz, i in place_all():
            at = dz * PLANE + i
            value = jnp.dot(both[m], value_of(ins, dz, i), preferred_element_type=jnp.float32)
            value = value * gain[at : at + 1, :]
            wide[came_from(place, dz, i)] = value
            top = jnp.maximum(top, jnp.abs(value))
        scale = jnp.max(top, axis=1, keepdims=True)
        scale_ref[...] = jnp.broadcast_to(scale, (cols, LANES)).T[0:1, :]
        down = 1.0 / scale
        copies = []
        for c in range(cols // 32):
            part = slice(c * 32, (c + 1) * 32)
            for p in range(PEERS):
                outbox[part, p * rows : (p + 1) * rows] = (wide[p, part] * down[part]).astype(
                    jnp.bfloat16
                )
            copies.append(pltpu.make_async_copy(outbox.at[part], final.at[part], outsem.at[c]))
            copies[-1].start()
        for copy in copies:
            copy.wait()

    return pl.pallas_call(
        kernel,
        in_specs=[VMEM] * (count + 2),
        out_specs=[HBM, VMEM],
        out_shape=[shape(cols, PEERS * rows), jax.ShapeDtypeStruct((1, cols), jnp.float32)],
        scratch_shapes=[
            pltpu.VMEM((PEERS, cols, rows), jnp.float32),
            pltpu.VMEM((cols, PEERS * rows), jnp.bfloat16),
            pltpu.SemaphoreType.DMA((cols // 32,)),
        ],
        compiler_params=PARAMS,
    )(*operands, gains, mix)


def on_device(
    w_query,
    low_query,
    high_query,
    w_key,
    low_key,
    high_key,
    w_value,
    low_value,
    high_value,
    norm_gain,
):
    cols = w_query.shape[1] // PEERS
    rank = low_query.shape[1]
    each = cols + rank
    first, rest = cols + EARLY, cols - EARLY
    models = lax.axis_size("model")

    def leg(part, dz, i):
        pairs = [(s, moved(s, dz, i)) for s in range(PEERS)]
        return lax.ppermute(part, "shard", pairs)

    def along_z(lot):
        return [lot[0], *(leg(lot[dz], dz, 0) for dz in range(1, SIDE))]

    def in_plane(lot):
        return [lot[0], *(leg(lot[i], 0, i) for i in range(1, PLANE))]

    lot_a, lot_b, lot_c, mix = pack(
        (w_query, w_key, w_value),
        (low_query.T, low_key.T, low_value.T),
        norm_gain,
        (high_query, high_key, high_value),
    )
    lot_a = along_z(lot_a)
    lot_b = in_plane(lot_b)
    lot_c = in_plane(lot_c)
    lot_b = along_z(repack_b(lot_b, cols, rank))
    moves = []
    for dz, i in place_all():
        to = dz * (each + EARLY)
        moves.append((i, to, dz, i * first, cols))
        moves.append((i, to + cols, dz, PLANE * first, rank))
        moves.append((i, to + each, dz, i * first + cols, EARLY))
    lot_a = repack(lot_a, moves, SIDE * (each + EARLY), PLANE)
    lot_a = in_plane(lot_a)
    moves = [(dz, i * rest, i, dz * rest, rest) for dz, i in place_all()]
    lot_c = repack(lot_c, moves, PLANE * rest, SIDE)
    lot_c = along_z(lot_c)
    mine, gains = collect(lot_b, cols, rank)
    theirs = lax.ppermute(mine, "model", [(m, m ^ 1) for m in range(models)])

    def adapter(refs, core, dz, i):
        at = (dz * PLANE + i) * rank
        own = lax.axis_index("model") % 2 == core
        return jnp.where(own, refs[0][at : at + rank, :], refs[1][at : at + rank, :])

    def value_of(refs, dz, i):
        weights = refs[dz][i * each : i * each + cols, :]
        return jnp.concatenate([weights, adapter(refs[SIDE:], 1, dz, i)], 0)

    def query_of(refs, dz, i):
        at = dz * (each + EARLY)
        return refs[i][at : at + each, :]

    def key_of(refs, dz, i):
        at = dz * (each + EARLY) + each
        early = refs[i][at : at + EARLY, :]
        late = refs[PLANE + dz][i * rest : (i + 1) * rest, :]
        return jnp.concatenate([early, late, adapter(refs[PLANE + SIDE :], 0, dz, i)], 0)

    final_v, scale_v = merge(value_of, 2, (*lot_b, mine, theirs), gains, mix)
    final_q, scale_q = merge(query_of, 0, lot_a, gains, mix)
    final_k, scale_k = merge(key_of, 1, (*lot_a, *lot_c, mine, theirs), gains, mix)
    return (
        final_q.T,
        final_k.T,
        final_v.T,
        scale_q.reshape(-1),
        scale_k.reshape(-1),
        scale_v.reshape(-1),
    )


def solution(mesh):
    return jax.shard_map(
        on_device,
        mesh=mesh,
        in_specs=(
            P("shard", "model"),
            P("shard", None),
            P(None, "model"),
            P("shard", "model"),
            P("shard", None),
            P(None, "model"),
            P("shard", "model"),
            P("shard", None),
            P(None, "model"),
            P("shard"),
        ),
        out_specs=(
            P(None, ("model", "shard")),
            P(None, ("model", "shard")),
            P(None, ("model", "shard")),
            P(("model", "shard")),
            P(("model", "shard")),
            P(("model", "shard")),
        ),
        check_vma=False,
    )
```

time: 157 us -> 205 us (1.31)
  waiting for transfers between devices: 68.8 us -> 134 us
  starting transfers between devices: 13.7 us -> 52.4 us
  blocking collectives: 28.5 us -> 0 us
  local copies, waits for them, and re-layouts: 22.7 us -> 0 us
  Pallas kernels: 0 us -> 17.7 us
  matrix products: 10.7 us -> 0 us
  other arithmetic: 10.7 us -> 0 us
    ppermute x0 -> x31, waiting for transfers between devices: none -> 134 us  [the longest x30 134 us: leg(): return lax.ppermute(part, 'shard', pairs)]
    all_to_all x3 -> x0, waiting for transfers between devices: 68.8 us -> none  [the longest x1 25.5 us: on_device(): lax.all_to_all(narrow_key, 'shard', split_axis=1, concat_axis=0, tiled=True)]
    ppermute x0 -> x31, starting transfers between devices: none -> 52.4 us  [the longest x30 52.3 us: leg(): return lax.ppermute(part, 'shard', pairs)]
    all_to_all x1 -> x0, blocking collectives: 28.5 us -> none  [sent_to_all(): return lax.all_to_all(copies, axis, split_axis=0, concat_axis=0, tiled=True)]
    pallas_call x0 -> x9, Pallas kernels: none -> 17.7 us  [the longest x3 8.86 us: merge(): pl.pallas_call(kernel, in_specs=[VMEM] * (count + 2), out_specs=[HBM, VME...]
    all_to_all x3 -> x0, starting transfers between devices: 13.7 us -> none  [the longest x1 4.8 us: on_device(): lax.all_to_all(narrow_value, 'shard', split_axis=1, concat_axis=0, tiled=...]
    convert_element_type x3 -> x0, local copies, waits for them, and re-layouts: 11 us -> none  [the longest x1 4.28 us: on_device(): (result_gained_key / scale_key).astype(jnp.bfloat16)]
    dot_general x3 -> x0, matrix products: 10.7 us -> none  [the longest x1 4.65 us: on_device(): jnp.dot(low_query, high_query, preferred_element_type=jnp.float32)]
  transfers between devices with their start and end apart: 3 -> 31, of which waited for: 3 -> 14; matrix products, arithmetic and copies ran while one was open for 15% -> 0% of each run, Pallas kernels for 0% -> 6%
where the time goes in v4:
time: 205 us
  waiting for transfers between devices  134 us (65%)
  starting transfers between devices  52.4 us (26%)
  Pallas kernels  17.7 us (9%)
    ppermute x30, waiting for transfers between devices, leg(): return lax.ppermute(part, 'shard', pairs)  134 us
    ppermute x30, starting transfers between devices, leg(): return lax.ppermute(part, 'shard', pairs)  52.3 us
    pallas_call x3, Pallas kernels, merge(): pl.pallas_call(kernel, in_specs=[VMEM] * (count + 2), out_specs=[HBM, VME...  8.86 us
    pallas_call x1, Pallas kernels, pack(): pl.pallas_call(functools.partial(pack_rest_kernel, cols=cols), in_specs=[...  5.33 us
  transfers between devices with their start and end apart: 31, of which 14 were waited for; matrix products, arithmetic and copies ran while one was open for 0% of the time, Pallas kernels for 6%

profile of v4, /device:TPU:0, one launch (start us, length us, event | category | flops | bytes accessed | tf_op | source)
XLA Modules:
  0.0 205.2 jit_solution(12496572793141017755)
XLA Ops:
  0.6 2.7 %pack_first.1 = (bf16[1296,384]{1,0:T(8,128)(2,1)S(1)}, bf16[408,384]{1,0:T(8,128)(2,1)S(1)}, bf16[408,384]{1,0:T(8,128)(2,1)S(1)}) custom-call(bf16[384,3072]{1,0:T(8,128)(2,1)} %wq.3, bf16[384,3072]{1,0:T(8,128)(2,1)} %wk.3, bf16[384,3072]{1,0:T(8,128)(2,1)} %wv.3, bf16[16,384]{1,0:T(8,128)(2,1)} %bitcast.9, bf16[16,384]{1,0:T(8,128)(2,1)} %bitcast.11, ...), custom_call_target="tpu_custom_call" | custom-call | tf_op jit(solution)/shard_map/pack_first/pallas_call | solution.py:219
  3.4 3.4 %collective-permute-start.13 = (bf16[408,384]{1,0:T(8,128)(2,1)S(1)}, bf16[408,384]{1,0:T(8,128)(2,1)S(1)}, u32[]{:S(2)}, u32[]{:S(2)}) collective-permute-start(bf16[408,384]{1,0:T(8,128)(2,1)S(1)} %get-tuple-element.67), channel_id=1, source_target_pairs={{0,16},{4,20},{8,24},{12,28},{16,0},{20,4},{24,8},{28,12},{32,48},... | collective-permute-start | bytes 940040 | tf_op jit(solution)/shard_map/ppermute | solution.py:405
  8.0 5.3 %pack_rest.1 = (bf16[1296,384]{1,0:T(8,128)(2,1)S(1)}, bf16[1296,384]{1,0:T(8,128)(2,1)S(1)}, bf16[1296,384]{1,0:T(8,128)(2,1)S(1)}, bf16[408,384]{1,0:T(8,128)(...) custom-call(bf16[384,3072]{1,0:T(8,128)(2,1)} %wq.3, ...), custom_call_target="tpu_custom_call" | custom-call | tf_op jit(solution)/shard_map/pack_rest/pallas_call | solution.py:243
  13.9 1.7 collective-permute-start.11
  15.6 2.5 %collective-permute-start.12 = (bf16[408,384]{1,0:T(8,128)(2,1)S(1)}, bf16[408,384]{1,0:T(8,128)(2,1)S(1)}, u32[]{:S(2)}, u32[]{:S(2)}) collective-permute-start(bf16[408,384]{1,0:T(8,128)(2,1)S(1)} %get-tuple-element.66), channel_id=1, source_target_pairs={{0,12},{4,8},{8,20},{12,16},{16,28},{20,24},{24,4},{28,0},{32,44},... | collective-permute-start | bytes 940040 | tf_op jit(solution)/shard_map/ppermute | solution.py:405
  18.1 4.3 %collective-permute-done.13.refs_4_ = bf16[408,384]{1,0:T(8,128)(2,1)S(1)} collective-permute-done((bf16[408,384]{1,0:T(8,128)(2,1)S(1)}, bf16[408,384]{1,0:T(8,128)(2,1)S(1)}, u32[]{:S(2)}, u32[]{:S(2)}) %collective-permute-start.13) | collective-permute-done | bytes 313376 | tf_op jit(solution)/shard_map/ppermute | solution.py:405
  23.9 3.9 %collective-permute-start.16 = (bf16[408,384]{1,0:T(8,128)(2,1)S(1)}, bf16[408,384]{1,0:T(8,128)(2,1)S(1)}, u32[]{:S(2)}, u32[]{:S(2)}) collective-permute-start(bf16[408,384]{1,0:T(8,128)(2,1)S(1)} %get-tuple-element.70), channel_id=1, source_target_pairs={{0,28},{4,24},{8,4},{12,0},{16,12},{20,8},{24,20},{28,16},{32,60},... | collective-permute-start | bytes 940040 | tf_op jit(solution)/shard_map/ppermute | solution.py:405
  27.9 6.4 %collective-permute-done.11.refs_2_ = bf16[408,384]{1,0:T(8,128)(2,1)S(1)} collective-permute-done((bf16[408,384]{1,0:T(8,128)(2,1)S(1)}, bf16[408,384]{1,0:T(8,128)(2,1)S(1)}, u32[]{:S(2)}, u32[]{:S(2)}) %collective-permute-start.11) | collective-permute-done | bytes 313376 | tf_op jit(solution)/shard_map/ppermute | solution.py:405
  34.3 2.2 %collective-permute-done.15.refs_6_ = bf16[408,384]{1,0:T(8,128)(2,1)S(1)} collective-permute-done((bf16[408,384]{1,0:T(8,128)(2,1)S(1)}, bf16[408,384]{1,0:T(8,128)(2,1)S(1)}, u32[]{:S(2)}, u32[]{:S(2)}) %collective-permute-start.15) | collective-permute-done | bytes 313376 | tf_op jit(solution)/shard_map/ppermute | solution.py:405
  36.9 2.0 collective-permute-start.17
  38.8 3.6 %collective-permute-start.1 = (bf16[1296,384]{1,0:T(8,128)(2,1)S(1)}, bf16[1296,384]{1,0:T(8,128)(2,1)S(1)}, u32[]{:S(2)}, u32[]{:S(2)}) collective-permute-start(bf16[1296,384]{1,0:T(8,128)(2,1)S(1)} %get-tuple-element.53), channel_id=1, source_target_pairs={{0,64},{4,68},{8,72},{12,76},{16,80},{20,84},{24,88},{28,92},{32,9... | collective-permute-start | bytes 2985992 | tf_op jit(solution)/shard_map/ppermute | solution.py:405
  42.4 3.2 %collective-permute-start.2 = (bf16[1296,384]{1,0:T(8,128)(2,1)S(1)}, bf16[1296,384]{1,0:T(8,128)(2,1)S(1)}, u32[]{:S(2)}, u32[]{:S(2)}) collective-permute-start(bf16[1296,384]{1,0:T(8,128)(2,1)S(1)} %get-tuple-element.54), channel_id=1, source_target_pairs={{0,96},{4,100},{8,104},{12,108},{16,112},{20,116},{24,120},{28,124... | collective-permute-start | bytes 2985992 | tf_op jit(solution)/shard_map/ppermute | solution.py:405
  45.7 31.8 %collective-permute-done.17.refs_1_ = bf16[920,384]{1,0:T(8,128)(2,1)S(1)} collective-permute-done((bf16[920,384]{1,0:T(8,128)(2,1)S(1)}, bf16[920,384]{1,0:T(8,128)(2,1)S(1)}, u32[]{:S(2)}, u32[]{:S(2)}) %collective-permute-start.17) | collective-permute-done | bytes 706592 | tf_op jit(solution)/shard_map/ppermute | solution.py:405
  77.5 37.1 %collective-permute-done.18.refs_2_ = bf16[920,384]{1,0:T(8,128)(2,1)S(1)} collective-permute-done((bf16[920,384]{1,0:T(8,128)(2,1)S(1)}, bf16[920,384]{1,0:T(8,128)(2,1)S(1)}, u32[]{:S(2)}, u32[]{:S(2)}) %collective-permute-start.18) | collective-permute-done | bytes 706592 | tf_op jit(solution)/shard_map/ppermute | solution.py:405
  114.5 2.0 collective-permute-start.20
  120.2 2.6 %collective-permute-start.22 = (bf16[128,384]{1,0:T(8,128)(2,1)S(1)}, bf16[128,384]{1,0:T(8,128)(2,1)S(1)}, u32[]{:S(2)}, u32[]{:S(2)}) collective-permute-start(bf16[128,384]{1,0:T(8,128)(2,1)S(1)} %get-tuple-element.81), channel_id=1, source_target_pairs={{0,12},{4,8},{8,20},{12,16},{16,28},{20,24},{24,4},{28,0},{32,44},... | collective-permute-start | bytes 294920 | tf_op jit(solution)/shard_map/ppermute | solution.py:405
  122.8 14.5 %collective-permute-done.21.refs_2_ = bf16[128,384]{1,0:T(8,128)(2,1)S(1)} collective-permute-done((bf16[128,384]{1,0:T(8,128)(2,1)S(1)}, bf16[128,384]{1,0:T(8,128)(2,1)S(1)}, u32[]{:S(2)}, u32[]{:S(2)}) %collective-permute-start.21) | collective-permute-done | bytes 98336 | tf_op jit(solution)/shard_map/ppermute | solution.py:405
  137.3 1.8 collective-permute-start.23
  139.1 2.8 %collective-permute-start.24 = (bf16[128,384]{1,0:T(8,128)(2,1)S(1)}, bf16[128,384]{1,0:T(8,128)(2,1)S(1)}, u32[]{:S(2)}, u32[]{:S(2)}) collective-permute-start(bf16[128,384]{1,0:T(8,128)(2,1)S(1)} %get-tuple-element.83), channel_id=1, source_target_pairs={{0,20},{4,16},{8,28},{12,24},{16,4},{20,0},{24,12},{28,8},{32,52},... | collective-permute-start | bytes 294920 | tf_op jit(solution)/shard_map/ppermute | solution.py:405
  144.0 2.1 %collective-permute-done.24.refs_5_ = bf16[128,384]{1,0:T(8,128)(2,1)S(1)} collective-permute-done((bf16[128,384]{1,0:T(8,128)(2,1)S(1)}, bf16[128,384]{1,0:T(8,128)(2,1)S(1)}, u32[]{:S(2)}, u32[]{:S(2)}) %collective-permute-start.24) | collective-permute-done | bytes 98336 | tf_op jit(solution)/shard_map/ppermute | solution.py:405
  146.1 2.5 %collective-permute-start.26 = (bf16[128,384]{1,0:T(8,128)(2,1)S(1)}, bf16[128,384]{1,0:T(8,128)(2,1)S(1)}, u32[]{:S(2)}, u32[]{:S(2)}) collective-permute-start(bf16[128,384]{1,0:T(8,128)(2,1)S(1)} %get-tuple-element.85), channel_id=1, source_target_pairs={{0,28},{4,24},{8,4},{12,0},{16,12},{20,8},{24,20},{28,16},{32,60},... | collective-permute-start | bytes 294920 | tf_op jit(solution)/shard_map/ppermute | solution.py:405
  149.7 2.1 %collective-permute-start.5 = (bf16[704,384]{1,0:T(8,128)(2,1)S(1)}, bf16[704,384]{1,0:T(8,128)(2,1)S(1)}, u32[]{:S(2)}, u32[]{:S(2)}) collective-permute-start(bf16[704,384]{1,0:T(8,128)(2,1)S(1)} %get-tuple-element.58), channel_id=1, source_target_pairs={{0,12},{4,8},{8,20},{12,16},{16,28},{20,24},{24,4},{28,0},{32,44},... | collective-permute-start | bytes 1622024 | tf_op jit(solution)/shard_map/ppermute | solution.py:405
  152.7 2.0 collective-permute-start.6
  154.7 2.6 %collective-permute-start.7 = (bf16[704,384]{1,0:T(8,128)(2,1)S(1)}, bf16[704,384]{1,0:T(8,128)(2,1)S(1)}, u32[]{:S(2)}, u32[]{:S(2)}) collective-permute-start(bf16[704,384]{1,0:T(8,128)(2,1)S(1)} %get-tuple-element.60), channel_id=1, source_target_pairs={{0,20},{4,16},{8,28},{12,24},{16,4},{20,0},{24,12},{28,8},{32,52},... | collective-permute-start | bytes 1622024 | tf_op jit(solution)/shard_map/ppermute | solution.py:405
  157.3 2.6 %collective-permute-start.8 = (bf16[704,384]{1,0:T(8,128)(2,1)S(1)}, bf16[704,384]{1,0:T(8,128)(2,1)S(1)}, u32[]{:S(2)}, u32[]{:S(2)}) collective-permute-start(bf16[704,384]{1,0:T(8,128)(2,1)S(1)} %get-tuple-element.61), channel_id=1, source_target_pairs={{0,24},{4,28},{8,0},{12,4},{16,8},{20,12},{24,16},{28,20},{32,56},... | collective-permute-start | bytes 1622024 | tf_op jit(solution)/shard_map/ppermute | solution.py:405
  160.0 7.5 %collective-permute-done.5.refs_3_ = bf16[704,384]{1,0:T(8,128)(2,1)S(1)} collective-permute-done((bf16[704,384]{1,0:T(8,128)(2,1)S(1)}, bf16[704,384]{1,0:T(8,128)(2,1)S(1)}, u32[]{:S(2)}, u32[]{:S(2)}) %collective-permute-start.5) | collective-permute-done | bytes 540704 | tf_op jit(solution)/shard_map/ppermute | solution.py:405
  168.2 18.9 %collective-permute-done.6.refs_4_ = bf16[704,384]{1,0:T(8,128)(2,1)S(1)} collective-permute-done((bf16[704,384]{1,0:T(8,128)(2,1)S(1)}, bf16[704,384]{1,0:T(8,128)(2,1)S(1)}, u32[]{:S(2)}, u32[]{:S(2)}) %collective-permute-start.6) | collective-permute-done | bytes 540704 | tf_op jit(solution)/shard_map/ppermute | solution.py:405
  188.4 2.0 collective-permute-start.29
  190.4 2.9 %shard_map.149 = (bf16[96,12288]{1,0:T(8,128)(2,1)}, f32[1,96]{1,0:T(1,128)}) custom-call(bf16[920,384]{1,0:T(8,128)(2,1)S(1)} %get-tuple-element.71.refs_0_, bf16[920,384]{1,0:T(8,128)(2,1)S(1)} %collective-permute-done.17.refs_1_, bf16[920,384]{1,0:T(8,128)(2,1)S(1)} %collective-permute-done.18.refs_2_, ...), custom_call_target="tpu_custom_call" | custom-call | tf_op jit(solution)/shard_map/pallas_call | solution.py:371
  193.3 5.7 %collective-permute-done.8.refs_6_ = bf16[704,384]{1,0:T(8,128)(2,1)S(1)} collective-permute-done((bf16[704,384]{1,0:T(8,128)(2,1)S(1)}, bf16[704,384]{1,0:T(8,128)(2,1)S(1)}, u32[]{:S(2)}, u32[]{:S(2)}) %collective-permute-start.8) | collective-permute-done | bytes 540704 | tf_op jit(solution)/shard_map/ppermute | solution.py:405
  199.0 3.0 %shard_map.146 = (bf16[96,12288]{1,0:T(8,128)(2,1)}, f32[1,96]{1,0:T(1,128)}) custom-call(bf16[704,384]{1,0:T(8,128)(2,1)S(1)} %get-tuple-element.55.refs_0_, bf16[704,384]{1,0:T(8,128)(2,1)S(1)} %collective-permute-done.3.refs_1_, bf16[704,384]{1,0:T(8,128)(2,1)S(1)} %collective-permute-done.4.refs_2_, bf16[704,384]{1,0:T(8,128)(2,1)S(1)} %collective-permute-done.5.refs_3_, ...), custom_call_target="tpu_custom_call" | custom-call | tf_op jit(solution)/shard_map/pallas_call | solution.py:371
  202.1 2.9 %shard_map.148 = (bf16[96,12288]{1,0:T(8,128)(2,1)}, f32[1,96]{1,0:T(1,128)}) custom-call(bf16[704,384]{1,0:T(8,128)(2,1)S(1)} %get-tuple-element.55.refs_0_, bf16[704,384]{1,0:T(8,128)(2,1)S(1)} %collective-permute-done.3.refs_1_, bf16[704,384]{1,0:T(8,128)(2,1)S(1)} %collective-permute-done.4.refs_2_, bf16[704,384]{1,0:T(8,128)(2,1)S(1)} %collective-permute-done.5.refs_3_, ...), custom_call_target="tpu_custom_call" | custom-call | tf_op jit(solution)/shard_map/pallas_call | solution.py:371
  (39 shorter events, 13.4 us)
Async XLA Ops:
  3.4 19.0 %collective-permute-start.13 = (bf16[408,384]{1,0:T(8,128)(2,1)S(1)}, bf16[408,384]{1,0:T(8,128)(2,1)S(1)}, u32[]{:S(2)}, u32[]{:S(2)}) collective-permute-start(bf16[408,384]{1,0:T(8,128)(2,1)S(1)} %get-tuple-element.67), channel_id=1, source_target_pairs={{0,16},{4,20},{8,24},{12,28},{16,0},{20,4},{24,8},{28,12},{32,48},... | collective-permute-start | bytes 940040 | tf_op jit(solution)/shard_map/ppermute | solution.py:405
  6.8 17.2 %collective-permute-start.14 = (bf16[408,384]{1,0:T(8,128)(2,1)S(1)}, bf16[408,384]{1,0:T(8,128)(2,1)S(1)}, u32[]{:S(2)}, u32[]{:S(2)}) collective-permute-start(bf16[408,384]{1,0:T(8,128)(2,1)S(1)} %get-tuple-element.68), channel_id=1, source_target_pairs={{0,20},{4,16},{8,28},{12,24},{16,4},{20,0},{24,12},{28,8},{32,52},... | collective-permute-start | bytes 940040 | tf_op jit(solution)/shard_map/ppermute | solution.py:405
  13.4 14.5 %collective-permute-start.10 = (bf16[408,384]{1,0:T(8,128)(2,1)S(1)}, bf16[408,384]{1,0:T(8,128)(2,1)S(1)}, u32[]{:S(2)}, u32[]{:S(2)}) collective-permute-start(bf16[408,384]{1,0:T(8,128)(2,1)S(1)} %get-tuple-element.64), channel_id=1, source_target_pairs={{0,4},{4,0},{8,12},{12,8},{16,20},{20,16},{24,28},{28,24},{32,36},... | collective-permute-start | bytes 940040 | tf_op jit(solution)/shard_map/ppermute | solution.py:405
  13.9 20.4 %collective-permute-start.11 = (bf16[408,384]{1,0:T(8,128)(2,1)S(1)}, bf16[408,384]{1,0:T(8,128)(2,1)S(1)}, u32[]{:S(2)}, u32[]{:S(2)}) collective-permute-start(bf16[408,384]{1,0:T(8,128)(2,1)S(1)} %get-tuple-element.65), channel_id=1, source_target_pairs={{0,8},{4,12},{8,16},{12,20},{16,24},{20,28},{24,0},{28,4},{32,40},... | collective-permute-start | bytes 940040 | tf_op jit(solution)/shard_map/ppermute | solution.py:405
  15.6 18.7 %collective-permute-start.12 = (bf16[408,384]{1,0:T(8,128)(2,1)S(1)}, bf16[408,384]{1,0:T(8,128)(2,1)S(1)}, u32[]{:S(2)}, u32[]{:S(2)}) collective-permute-start(bf16[408,384]{1,0:T(8,128)(2,1)S(1)} %get-tuple-element.66), channel_id=1, source_target_pairs={{0,12},{4,8},{8,20},{12,16},{16,28},{20,24},{24,4},{28,0},{32,44},... | collective-permute-start | bytes 940040 | tf_op jit(solution)/shard_map/ppermute | solution.py:405
  22.4 14.1 %collective-permute-start.15 = (bf16[408,384]{1,0:T(8,128)(2,1)S(1)}, bf16[408,384]{1,0:T(8,128)(2,1)S(1)}, u32[]{:S(2)}, u32[]{:S(2)}) collective-permute-start(bf16[408,384]{1,0:T(8,128)(2,1)S(1)} %get-tuple-element.69), channel_id=1, source_target_pairs={{0,24},{4,28},{8,0},{12,4},{16,8},{20,12},{24,16},{28,20},{32,56},... | collective-permute-start | bytes 940040 | tf_op jit(solution)/shard_map/ppermute | solution.py:405
  23.9 12.7 %collective-permute-start.16 = (bf16[408,384]{1,0:T(8,128)(2,1)S(1)}, bf16[408,384]{1,0:T(8,128)(2,1)S(1)}, u32[]{:S(2)}, u32[]{:S(2)}) collective-permute-start(bf16[408,384]{1,0:T(8,128)(2,1)S(1)} %get-tuple-element.70), channel_id=1, source_target_pairs={{0,28},{4,24},{8,4},{12,0},{16,12},{20,8},{24,20},{28,16},{32,60},... | collective-permute-start | bytes 940040 | tf_op jit(solution)/shard_map/ppermute | solution.py:405
  36.9 40.6 %collective-permute-start.17 = (bf16[920,384]{1,0:T(8,128)(2,1)S(1)}, bf16[920,384]{1,0:T(8,128)(2,1)S(1)}, u32[]{:S(2)}, u32[]{:S(2)}) collective-permute-start(bf16[920,384]{1,0:T(8,128)(2,1)S(1)} %get-tuple-element.72), channel_id=1, source_target_pairs={{0,32},{4,36},{8,40},{12,44},{16,48},{20,52},{24,56},{28,60},{32,6... | collective-permute-start | bytes 2119688 | tf_op jit(solution)/shard_map/ppermute | solution.py:405
  38.8 77.8 %collective-permute-start.1 = (bf16[1296,384]{1,0:T(8,128)(2,1)S(1)}, bf16[1296,384]{1,0:T(8,128)(2,1)S(1)}, u32[]{:S(2)}, u32[]{:S(2)}) collective-permute-start(bf16[1296,384]{1,0:T(8,128)(2,1)S(1)} %get-tuple-element.53), channel_id=1, source_target_pairs={{0,64},{4,68},{8,72},{12,76},{16,80},{20,84},{24,88},{28,92},{32,9... | collective-permute-start | bytes 2985992 | tf_op jit(solution)/shard_map/ppermute | solution.py:405
  42.4 74.2 %collective-permute-start = (bf16[1296,384]{1,0:T(8,128)(2,1)S(1)}, bf16[1296,384]{1,0:T(8,128)(2,1)S(1)}, u32[]{:S(2)}, u32[]{:S(2)}) collective-permute-start(bf16[1296,384]{1,0:T(8,128)(2,1)S(1)} %get-tuple-element.52), channel_id=1, source_target_pairs={{0,32},{4,36},{8,40},{12,44},{16,48},{20,52},{24,56},{28,60},{32,6... | collective-permute-start | bytes 2985992 | tf_op jit(solution)/shard_map/ppermute | solution.py:405
  42.4 74.2 %collective-permute-start.2 = (bf16[1296,384]{1,0:T(8,128)(2,1)S(1)}, bf16[1296,384]{1,0:T(8,128)(2,1)S(1)}, u32[]{:S(2)}, u32[]{:S(2)}) collective-permute-start(bf16[1296,384]{1,0:T(8,128)(2,1)S(1)} %get-tuple-element.54), channel_id=1, source_target_pairs={{0,96},{4,100},{8,104},{12,108},{16,112},{20,116},{24,120},{28,124... | collective-permute-start | bytes 2985992 | tf_op jit(solution)/shard_map/ppermute | solution.py:405
  45.7 68.9 %collective-permute-start.18 = (bf16[920,384]{1,0:T(8,128)(2,1)S(1)}, bf16[920,384]{1,0:T(8,128)(2,1)S(1)}, u32[]{:S(2)}, u32[]{:S(2)}) collective-permute-start(bf16[920,384]{1,0:T(8,128)(2,1)S(1)} %get-tuple-element.73), channel_id=1, source_target_pairs={{0,64},{4,68},{8,72},{12,76},{16,80},{20,84},{24,88},{28,92},{32,9... | collective-permute-start | bytes 2119688 | tf_op jit(solution)/shard_map/ppermute | solution.py:405
  77.5 39.0 %collective-permute-start.19 = (bf16[920,384]{1,0:T(8,128)(2,1)S(1)}, bf16[920,384]{1,0:T(8,128)(2,1)S(1)}, u32[]{:S(2)}, u32[]{:S(2)}) collective-permute-start(bf16[920,384]{1,0:T(8,128)(2,1)S(1)} %get-tuple-element.74), channel_id=1, source_target_pairs={{0,96},{4,100},{8,104},{12,108},{16,112},{20,116},{24,120},{28,124... | collective-permute-start | bytes 2119688 | tf_op jit(solution)/shard_map/ppermute | solution.py:405
  114.5 5.6 %collective-permute-start.20 = (bf16[128,384]{1,0:T(8,128)(2,1)S(1)}, bf16[128,384]{1,0:T(8,128)(2,1)S(1)}, u32[]{:S(2)}, u32[]{:S(2)}) collective-permute-start(bf16[128,384]{1,0:T(8,128)(2,1)S(1)} %get-tuple-element.79), channel_id=1, source_target_pairs={{0,4},{4,0},{8,12},{12,8},{16,20},{20,16},{24,28},{28,24},{32,36},... | collective-permute-start | bytes 294920 | tf_op jit(solution)/shard_map/ppermute | solution.py:405
  116.5 38.1 %collective-permute-start.30 = (bf16[512,384]{1,0:T(8,128)(2,1)S(1)}, bf16[512,384]{1,0:T(8,128)(2,1)S(1)}, u32[]{:S(2)}, u32[]{:S(2)}) collective-permute-start(bf16[512,384]{1,0:T(8,128)(2,1)S(1)} %get-tuple-element.90.refs_12_.refs_4_), channel_id=1, source_target_pairs={{0,1},{1,0},{2,3},{3,2},{4,5},{5,4},{6,7},{7,6},{8,9},{9,8},{10,11... | collective-permute-start | bytes 1179656 | tf_op jit(solution)/shard_map/ppermute | solution.py:435
  117.1 40.3 %collective-permute-start.3 = (bf16[704,384]{1,0:T(8,128)(2,1)S(1)}, bf16[704,384]{1,0:T(8,128)(2,1)S(1)}, u32[]{:S(2)}, u32[]{:S(2)}) collective-permute-start(bf16[704,384]{1,0:T(8,128)(2,1)S(1)} %get-tuple-element.56), channel_id=1, source_target_pairs={{0,4},{4,0},{8,12},{12,8},{16,20},{20,16},{24,28},{28,24},{32,36},... | collective-permute-start | bytes 1622024 | tf_op jit(solution)/shard_map/ppermute | solution.py:405
  117.2 42.7 %collective-permute-start.4 = (bf16[704,384]{1,0:T(8,128)(2,1)S(1)}, bf16[704,384]{1,0:T(8,128)(2,1)S(1)}, u32[]{:S(2)}, u32[]{:S(2)}) collective-permute-start(bf16[704,384]{1,0:T(8,128)(2,1)S(1)} %get-tuple-element.57), channel_id=1, source_target_pairs={{0,8},{4,12},{8,16},{12,20},{16,24},{20,28},{24,0},{28,4},{32,40},... | collective-permute-start | bytes 1622024 | tf_op jit(solution)/shard_map/ppermute | solution.py:405
  118.9 18.4 %collective-permute-start.21 = (bf16[128,384]{1,0:T(8,128)(2,1)S(1)}, bf16[128,384]{1,0:T(8,128)(2,1)S(1)}, u32[]{:S(2)}, u32[]{:S(2)}) collective-permute-start(bf16[128,384]{1,0:T(8,128)(2,1)S(1)} %get-tuple-element.80), channel_id=1, source_target_pairs={{0,8},{4,12},{8,16},{12,20},{16,24},{20,28},{24,0},{28,4},{32,40},... | collective-permute-start | bytes 294920 | tf_op jit(solution)/shard_map/ppermute | solution.py:405
  120.2 18.9 %collective-permute-start.22 = (bf16[128,384]{1,0:T(8,128)(2,1)S(1)}, bf16[128,384]{1,0:T(8,128)(2,1)S(1)}, u32[]{:S(2)}, u32[]{:S(2)}) collective-permute-start(bf16[128,384]{1,0:T(8,128)(2,1)S(1)} %get-tuple-element.81), channel_id=1, source_target_pairs={{0,12},{4,8},{8,20},{12,16},{16,28},{20,24},{24,4},{28,0},{32,44},... | collective-permute-start | bytes 294920 | tf_op jit(solution)/shard_map/ppermute | solution.py:405
  137.3 6.1 %collective-permute-start.23 = (bf16[128,384]{1,0:T(8,128)(2,1)S(1)}, bf16[128,384]{1,0:T(8,128)(2,1)S(1)}, u32[]{:S(2)}, u32[]{:S(2)}) collective-permute-start(bf16[128,384]{1,0:T(8,128)(2,1)S(1)} %get-tuple-element.82), channel_id=1, source_target_pairs={{0,16},{4,20},{8,24},{12,28},{16,0},{20,4},{24,8},{28,12},{32,48},... | collective-permute-start | bytes 294920 | tf_op jit(solution)/shard_map/ppermute | solution.py:405
  139.1 7.0 %collective-permute-start.24 = (bf16[128,384]{1,0:T(8,128)(2,1)S(1)}, bf16[128,384]{1,0:T(8,128)(2,1)S(1)}, u32[]{:S(2)}, u32[]{:S(2)}) collective-permute-start(bf16[128,384]{1,0:T(8,128)(2,1)S(1)} %get-tuple-element.83), channel_id=1, source_target_pairs={{0,20},{4,16},{8,28},{12,24},{16,4},{20,0},{24,12},{28,8},{32,52},... | collective-permute-start | bytes 294920 | tf_op jit(solution)/shard_map/ppermute | solution.py:405
  143.4 6.3 %collective-permute-start.25 = (bf16[128,384]{1,0:T(8,128)(2,1)S(1)}, bf16[128,384]{1,0:T(8,128)(2,1)S(1)}, u32[]{:S(2)}, u32[]{:S(2)}) collective-permute-start(bf16[128,384]{1,0:T(8,128)(2,1)S(1)} %get-tuple-element.84), channel_id=1, source_target_pairs={{0,24},{4,28},{8,0},{12,4},{16,8},{20,12},{24,16},{28,20},{32,56},... | collective-permute-start | bytes 294920 | tf_op jit(solution)/shard_map/ppermute | solution.py:405
  146.1 6.6 %collective-permute-start.26 = (bf16[128,384]{1,0:T(8,128)(2,1)S(1)}, bf16[128,384]{1,0:T(8,128)(2,1)S(1)}, u32[]{:S(2)}, u32[]{:S(2)}) collective-permute-start(bf16[128,384]{1,0:T(8,128)(2,1)S(1)} %get-tuple-element.85), channel_id=1, source_target_pairs={{0,28},{4,24},{8,4},{12,0},{16,12},{20,8},{24,20},{28,16},{32,60},... | collective-permute-start | bytes 294920 | tf_op jit(solution)/shard_map/ppermute | solution.py:405
  149.7 17.8 %collective-permute-start.5 = (bf16[704,384]{1,0:T(8,128)(2,1)S(1)}, bf16[704,384]{1,0:T(8,128)(2,1)S(1)}, u32[]{:S(2)}, u32[]{:S(2)}) collective-permute-start(bf16[704,384]{1,0:T(8,128)(2,1)S(1)} %get-tuple-element.58), channel_id=1, source_target_pairs={{0,12},{4,8},{8,20},{12,16},{16,28},{20,24},{24,4},{28,0},{32,44},... | collective-permute-start | bytes 1622024 | tf_op jit(solution)/shard_map/ppermute | solution.py:405
  152.7 34.5 %collective-permute-start.6 = (bf16[704,384]{1,0:T(8,128)(2,1)S(1)}, bf16[704,384]{1,0:T(8,128)(2,1)S(1)}, u32[]{:S(2)}, u32[]{:S(2)}) collective-permute-start(bf16[704,384]{1,0:T(8,128)(2,1)S(1)} %get-tuple-element.59), channel_id=1, source_target_pairs={{0,16},{4,20},{8,24},{12,28},{16,0},{20,4},{24,8},{28,12},{32,48},... | collective-permute-start | bytes 1622024 | tf_op jit(solution)/shard_map/ppermute | solution.py:405
  154.7 33.7 %collective-permute-start.7 = (bf16[704,384]{1,0:T(8,128)(2,1)S(1)}, bf16[704,384]{1,0:T(8,128)(2,1)S(1)}, u32[]{:S(2)}, u32[]{:S(2)}) collective-permute-start(bf16[704,384]{1,0:T(8,128)(2,1)S(1)} %get-tuple-element.60), channel_id=1, source_target_pairs={{0,20},{4,16},{8,28},{12,24},{16,4},{20,0},{24,12},{28,8},{32,52},... | collective-permute-start | bytes 1622024 | tf_op jit(solution)/shard_map/ppermute | solution.py:405
  157.3 41.7 %collective-permute-start.8 = (bf16[704,384]{1,0:T(8,128)(2,1)S(1)}, bf16[704,384]{1,0:T(8,128)(2,1)S(1)}, u32[]{:S(2)}, u32[]{:S(2)}) collective-permute-start(bf16[704,384]{1,0:T(8,128)(2,1)S(1)} %get-tuple-element.61), channel_id=1, source_target_pairs={{0,24},{4,28},{8,0},{12,4},{16,8},{20,12},{24,16},{28,20},{32,56},... | collective-permute-start | bytes 1622024 | tf_op jit(solution)/shard_map/ppermute | solution.py:405
  159.9 39.1 %collective-permute-start.9 = (bf16[704,384]{1,0:T(8,128)(2,1)S(1)}, bf16[704,384]{1,0:T(8,128)(2,1)S(1)}, u32[]{:S(2)}, u32[]{:S(2)}) collective-permute-start(bf16[704,384]{1,0:T(8,128)(2,1)S(1)} %get-tuple-element.62), channel_id=1, source_target_pairs={{0,28},{4,24},{8,4},{12,0},{16,12},{20,8},{24,20},{28,16},{32,60},... | collective-permute-start | bytes 1622024 | tf_op jit(solution)/shard_map/ppermute | solution.py:405
  167.5 34.5 %collective-permute-start.27 = (bf16[256,384]{1,0:T(8,128)(2,1)S(1)}, bf16[256,384]{1,0:T(8,128)(2,1)S(1)}, u32[]{:S(2)}, u32[]{:S(2)}) collective-permute-start(bf16[256,384]{1,0:T(8,128)(2,1)S(1)} %get-tuple-element.87), channel_id=1, source_target_pairs={{0,32},{4,36},{8,40},{12,44},{16,48},{20,52},{24,56},{28,60},{32,6... | collective-permute-start | bytes 589832 | tf_op jit(solution)/shard_map/ppermute | solution.py:405
  187.1 14.9 %collective-permute-start.28 = (bf16[256,384]{1,0:T(8,128)(2,1)S(1)}, bf16[256,384]{1,0:T(8,128)(2,1)S(1)}, u32[]{:S(2)}, u32[]{:S(2)}) collective-permute-start(bf16[256,384]{1,0:T(8,128)(2,1)S(1)} %get-tuple-element.88), channel_id=1, source_target_pairs={{0,64},{4,68},{8,72},{12,76},{16,80},{20,84},{24,88},{28,92},{32,9... | collective-permute-start | bytes 589832 | tf_op jit(solution)/shard_map/ppermute | solution.py:405
  188.4 13.7 %collective-permute-start.29 = (bf16[256,384]{1,0:T(8,128)(2,1)S(1)}, bf16[256,384]{1,0:T(8,128)(2,1)S(1)}, u32[]{:S(2)}, u32[]{:S(2)}) collective-permute-start(bf16[256,384]{1,0:T(8,128)(2,1)S(1)} %get-tuple-element.89), channel_id=1, source_target_pairs={{0,96},{4,100},{8,104},{12,108},{16,112},{20,116},{24,120},{28,124... | collective-permute-start | bytes 589832 | tf_op jit(solution)/shard_map/ppermute | solution.py:405
